TPU v7x, 8 devices: a whole 2x2x1 slice. The times are simulated.
8 devices in a mesh: problem: 1 (over z), samp: 2 (over y), feat: 4 (over x, core).
Axes of the slice: x: 2, y: 2, z: 1, core: 2. Of those that a mesh axis runs over, the one named last changes fastest.
Arguments:
- design: bfloat16 [16384, 16384], P(('problem', 'samp'), 'feat')
- targets: float32 [16384, 256], P(('problem', 'samp'))
- coef_init: float32 [16384, 256], P(('problem', 'feat'))
- step_sizes: float32 [16384], P(('problem', 'feat'))
- ridge_weights: float32 [256], P('problem')
Outputs:
- output 1: float32 [16384, 256], P(('problem', 'feat'))
- output 2: float32 [16384, 256], P(('problem', 'samp'))
All inputs are finite; a program needn't handle non-finite values.
Results may differ from a plain program's by a relative error of at most 0.00678921.
Values are sent between devices in bfloat16 or wider.
A program may use at most 1 GiB of HBM per device.

v0:
```python
import jax
import jax.numpy as jnp
from jax import lax
from jax.sharding import PartitionSpec as P

SWEEPS = 4
STEP_WEIGHT = 0.5


def solution(mesh):
    samp_size = mesh.shape["samp"]
    design_spec = P(("problem", "samp"), "feat")
    rows_spec = P(("problem", "samp"), None)
    coef_spec = P(("problem", "feat"), None)
    step_spec = P(("problem", "feat"))
    ridge_spec = P("problem")

    def local_sweeps(design, targets, coef_init, step_sizes, ridge_weights):
        total_rows = design.shape[0] * samp_size
        step_col = step_sizes[:, None]
        ridge_row = ridge_weights[None, :]

        def block_product(weights):
            product = jnp.dot(design, weights.astype(jnp.bfloat16), preferred_element_type=jnp.float32)
            return product.astype(jnp.bfloat16).astype(jnp.float32)

        resid_cur = targets - lax.psum(block_product(coef_init), "feat")
        coef_cur = coef_init
        for sweep_index in range(SWEEPS):
            part_grad = lax.dot_general(design, resid_cur.astype(jnp.bfloat16), (((0,), (0,)), ((), ())), preferred_element_type=jnp.float32)
            gradient = lax.psum(part_grad, "samp") / total_rows
            step_delta = step_col * (gradient - ridge_row * coef_cur)
            coef_cur = coef_cur + STEP_WEIGHT * step_delta
            resid_cur = resid_cur - STEP_WEIGHT * lax.psum(block_product(step_delta), "feat")
        return coef_cur, resid_cur

    return jax.shard_map(local_sweeps, mesh=mesh, in_specs=(design_spec, rows_spec, coef_spec, step_spec, ridge_spec), out_specs=(coef_spec, rows_spec), check_vma=False)
```

profile of v0, /device:TPU:0, one launch (start us, length us, event | category | flops | bytes accessed | tf_op | source)
XLA Modules:
  0.0 1487.1 jit_solution(4112938832843853484)
XLA Ops:
  7.2 30.1 %fusion = f32[8192,256]{1,0:T(8,128)} fusion(bf16[8192,4096]{1,0:T(8,128)(2,1)} %param.5, f32[4096,256]{1,0:T(8,128)} %param.7), kind=kOutput, calls=%fused_computation.5 | convolution fusion | flops 17185112064 | bytes 79691776 | tf_op jit(solution)/shard_map/dot_general | solution.py:24
  37.9 149.5 %all-reduce.10.cloned.1.call-done = f32[8192,256]{1,0:T(8,128)} async-done(((f32[8192,256]{1,0:T(8,128)}), f32[8192,256]{1,0:T(8,128)}) %all-reduce.10.cloned.1.call-update) | async-done | bytes 8388624 | tf_op jit(solution)/shard_map/psum | solution.py:27
  187.4 10.2 sub.27
  197.7 31.0 %convolution_bitcast_fusion.3 = f32[4096,256]{0,1:T(8,128)} fusion(bf16[8192,4096]{1,0:T(8,128)(2,1)} %param.5, f32[8192,256]{1,0:T(8,128)} %sub.27), kind=kOutput, calls=%fused_computation.21 | convolution fusion | flops 17181966336 | bytes 79691776 | tf_op jit(solution)/shard_map/dot_general | solution.py:30
  228.8 5.6 copy.8
  234.4 96.7 %all-reduce.12.cloned.1.call-done = f32[4096,256]{0,1:T(8,128)} async-done(((f32[4096,256]{0,1:T(8,128)}), f32[4096,256]{0,1:T(8,128)}) %all-reduce.12.cloned.1.call-update) | async-done | bytes 4194320 | tf_op jit(solution)/shard_map/psum | solution.py:31
  331.1 32.2 %fusion.2 = f32[8192,256]{1,0:T(8,128)} fusion(bf16[8192,4096]{1,0:T(8,128)(2,1)} %param.5, f32[4096,256]{0,1:T(8,128)} %copy.8, f32[4096,256]{0,1:T(8,128)} %all-reduce.12.cloned.1.call-done, f32[256]{0:T(256)S(1)} %copy-done.1, f32[4096]{0:T(1024)S(1)} %copy-done), kind=kOutput, calls=%fused_computation.7 | convolution fusion | flops 17189306368 | bytes 83903488 | tf_op jit(solution)/shard_map/dot_general | solution.py:24
  363.5 147.0 %all-reduce.14.cloned.1.call-done = f32[8192,256]{1,0:T(8,128)} async-done(((f32[8192,256]{1,0:T(8,128)}), f32[8192,256]{1,0:T(8,128)}) %all-reduce.14.cloned.1.call-update) | async-done | bytes 8388624 | tf_op jit(solution)/shard_map/psum | solution.py:34
  510.6 32.3 %convolution_bitcast_fusion.2 = f32[4096,256]{0,1:T(8,128)} fusion(bf16[8192,4096]{1,0:T(8,128)(2,1)} %param.5, f32[8192,256]{1,0:T(8,128)} %sub.27, f32[8192,256]{1,0:T(8,128)} %all-reduce.14.cloned.1.call-done), kind=kOutput, calls=%fused_computation.20 | convolution fusion | flops 17186160640 | bytes 88080384 | tf_op jit(solution)/shard_map/dot_general | solution.py:30
  542.9 102.3 %all-reduce.16.cloned.1.call-done = f32[4096,256]{0,1:T(8,128)} async-done(((f32[4096,256]{0,1:T(8,128)}), f32[4096,256]{0,1:T(8,128)}) %all-reduce.16.cloned.1.call-update) | async-done | bytes 4194320 | tf_op jit(solution)/shard_map/psum | solution.py:31
  645.2 33.9 %fusion.4 = f32[8192,256]{1,0:T(8,128)} fusion(bf16[8192,4096]{1,0:T(8,128)(2,1)} %param.5, f32[4096,256]{0,1:T(8,128)} %all-reduce.16.cloned.1.call-done, f32[256]{0:T(256)S(1)} %copy-done.1, f32[4096]{0:T(1024)S(1)} %copy-done, f32[4096,256]{0,1:T(8,128)} %copy.8, f32[4096,256]{0,1:T(8,128)} %all-reduce.12.cloned.1.call-done), kind=kOutput, calls=%fused_computation.9 | convolution fusion | flops 17195597824 | bytes 88097792 | tf_op jit(solution)/shard_map/dot_general | solution.py:24
  679.4 147.0 %all-reduce.18.cloned.1.call-done = f32[8192,256]{1,0:T(8,128)} async-done(((f32[8192,256]{1,0:T(8,128)}), f32[8192,256]{1,0:T(8,128)}) %all-reduce.18.cloned.1.call-update) | async-done | bytes 8388624 | tf_op jit(solution)/shard_map/psum | solution.py:34
  826.4 12.6 multiply_subtract_fusion.2
  839.0 31.0 %convolution_bitcast_fusion.1 = f32[4096,256]{0,1:T(8,128)} fusion(bf16[8192,4096]{1,0:T(8,128)(2,1)} %param.5, f32[8192,256]{1,0:T(8,128)} %multiply_subtract_fusion.2), kind=kOutput, calls=%fused_computation.19 | convolution fusion | flops 17181966336 | bytes 79691776 | tf_op jit(solution)/shard_map/dot_general | solution.py:30
  870.1 6.9 multiply_add_fusion.2
  877.0 95.5 %all-reduce.20.cloned.1.call-done = f32[4096,256]{0,1:T(8,128)} async-done(((f32[4096,256]{0,1:T(8,128)}), f32[4096,256]{0,1:T(8,128)}) %all-reduce.20.cloned.1.call-update) | async-done | bytes 4194320 | tf_op jit(solution)/shard_map/psum | solution.py:31
  972.4 32.2 %fusion.6 = f32[8192,256]{1,0:T(8,128)} fusion(bf16[8192,4096]{1,0:T(8,128)(2,1)} %param.5, f32[4096,256]{0,1:T(8,128)} %multiply_add_fusion.2, f32[4096,256]{0,1:T(8,128)} %all-reduce.20.cloned.1.call-done, f32[256]{0:T(256)S(1)} %copy-done.1, f32[4096]{0:T(1024)S(1)} %copy-done), kind=kOutput, calls=%fused_computation.11 | convolution fusion | flops 17189306368 | bytes 83903488 | tf_op jit(solution)/shard_map/dot_general | solution.py:24
  1004.9 147.0 %all-reduce.22.cloned.1.call-done = f32[8192,256]{1,0:T(8,128)} async-done(((f32[8192,256]{1,0:T(8,128)}), f32[8192,256]{1,0:T(8,128)}) %all-reduce.22.cloned.1.call-update) | async-done | bytes 8388624 | tf_op jit(solution)/shard_map/psum | solution.py:34
  1151.9 32.2 %convolution_bitcast_fusion = f32[4096,256]{0,1:T(8,128)} fusion(bf16[8192,4096]{1,0:T(8,128)(2,1)} %param.5, f32[8192,256]{1,0:T(8,128)} %multiply_subtract_fusion.2, f32[8192,256]{1,0:T(8,128)} %all-reduce.22.cloned.1.call-done), kind=kOutput, calls=%fused_computation.18 | convolution fusion | flops 17186160640 | bytes 88080384 | tf_op jit(solution)/shard_map/dot_general | solution.py:30
  1184.2 102.3 %all-reduce.24.cloned.1.call-done = f32[4096,256]{0,1:T(8,128)} async-done(((f32[4096,256]{0,1:T(8,128)}), f32[4096,256]{0,1:T(8,128)}) %all-reduce.24.cloned.1.call-update) | async-done | bytes 4194320 | tf_op jit(solution)/shard_map/psum | solution.py:31
  1286.5 33.9 %fusion.8 = f32[8192,256]{1,0:T(8,128)} fusion(bf16[8192,4096]{1,0:T(8,128)(2,1)} %param.5, f32[4096,256]{0,1:T(8,128)} %all-reduce.24.cloned.1.call-done, f32[256]{0:T(256)S(1)} %copy-done.1, f32[4096]{0:T(1024)S(1)} %copy-done, f32[4096,256]{0,1:T(8,128)} %multiply_add_fusion.2, f32[4096,256]{0,1:T(8,128)} %all-reduce.20.cloned.1.call-done), kind=kOutput, calls=%fused_computation.13 | convolution fusion | flops 17195597824 | bytes 88097792 | tf_op jit(solution)/shard_map/dot_general | solution.py:24
  1320.4 6.9 multiply_add_fusion
  1332.9 134.8 %all-reduce.26.cloned.1.call-done = f32[8192,256]{1,0:T(8,128)} async-done(((f32[8192,256]{1,0:T(8,128)}), f32[8192,256]{1,0:T(8,128)}) %all-reduce.26.cloned.1.call-update) | async-done | bytes 8388624 | tf_op jit(solution)/shard_map/psum | solution.py:34
  1467.7 12.6 multiply_subtract_fusion
  (23 shorter events, 7.3 us)
Async XLA Ops:
  7.2 180.2 %all-reduce.10.cloned.1.call-start = ((), (), s32[]{:S(2)}) async-start(), calls=%async_computation | async-start | bytes 16777216 | tf_op jit(solution)/shard_map/psum | solution.py:27
  37.3 293.8 %all-reduce.12.cloned.1.call-start = ((), (), s32[]{:S(2)}) async-start(), calls=%async_computation.1 | async-start | bytes 8388608 | tf_op jit(solution)/shard_map/psum | solution.py:31
  228.7 102.4 %copy-start = (f32[4096]{0:T(1024)S(1)}, f32[4096]{0:T(1024)}, u32[]{:S(2)}) copy-start(f32[4096]{0:T(1024)} %param.8) | copy-start | bytes 49156
  228.7 102.4 %copy-start.1 = (f32[256]{0:T(256)S(1)}, f32[256]{0:T(256)}, u32[]{:S(2)}) copy-start(f32[256]{0:T(256)} %param.9) | copy-start | bytes 3076
  228.7 281.8 %all-reduce.14.cloned.1.call-start = ((), (), s32[]{:S(2)}) async-start(), calls=%async_computation.2 | async-start | bytes 16777216 | tf_op jit(solution)/shard_map/psum | solution.py:34
  363.3 281.9 %all-reduce.16.cloned.1.call-start = ((), (), s32[]{:S(2)}) async-start(), calls=%async_computation.3 | async-start | bytes 8388608 | tf_op jit(solution)/shard_map/psum | solution.py:31
  542.8 283.6 %all-reduce.18.cloned.1.call-start = ((), (), s32[]{:S(2)}) async-start(), calls=%async_computation.4 | async-start | bytes 16777216 | tf_op jit(solution)/shard_map/psum | solution.py:34
  679.1 293.3 %all-reduce.20.cloned.1.call-start = ((), (), s32[]{:S(2)}) async-start(), calls=%async_computation.5 | async-start | bytes 8388608 | tf_op jit(solution)/shard_map/psum | solution.py:31
  870.0 281.9 %all-reduce.22.cloned.1.call-start = ((), (), s32[]{:S(2)}) async-start(), calls=%async_computation.6 | async-start | bytes 16777216 | tf_op jit(solution)/shard_map/psum | solution.py:34
  1004.6 281.9 %all-reduce.24.cloned.1.call-start = ((), (), s32[]{:S(2)}) async-start(), calls=%async_computation.7 | async-start | bytes 8388608 | tf_op jit(solution)/shard_map/psum | solution.py:31
  1184.1 283.5 %all-reduce.26.cloned.1.call-start = ((), (), s32[]{:S(2)}) async-start(), calls=%async_computation.8 | async-start | bytes 16777216 | tf_op jit(solution)/shard_map/psum | solution.py:34
Sparse Core Ops, SparseCore 0:
  37.4 149.9 all-reduce.9
  228.8 102.2 all-reduce.11
  363.4 147.0 all-reduce.13
  543.0 102.2 all-reduce.15
  679.3 147.1 all-reduce.17
  870.1 102.2 all-reduce.19
  1004.7 147.1 all-reduce.21
  1184.3 102.2 all-reduce.23
  1320.5 147.1 all-reduce.25
where the time goes:
time: 1490 us
  waiting for transfers between devices  1120 us (75%)
  matrix products  289 us (19%)
  other arithmetic  49.2 us (3%)
    psum x4, waiting for transfers between devices, local_sweeps(): lax.psum(block_product(step_delta), 'feat')  576 us
    psum x4, waiting for transfers between devices, local_sweeps(): gradient = lax.psum(part_grad, 'samp') / total_rows  397 us
    dot_general x5, matrix products, block_product(): jnp.dot(design, weights.astype(jnp.bfloat16), preferred_element_type=jnp....  162 us
    psum x1, waiting for transfers between devices, local_sweeps(): resid_cur = targets - lax.psum(block_product(coef_init), 'feat')  150 us
    dot_general x4, matrix products, local_sweeps(): lax.dot_general(design, resid_cur.astype(jnp.bfloat16), (((0,), (0,)), ((...  127 us
  transfers between devices with their start and end apart: 9, of which 9 were waited for; matrix products, arithmetic and copies ran while one was open for 2% of the time, Pallas kernels for 0%

commit v1 on v0

v1 whole, which is shorter than its diff:
```python
import functools

import jax
import jax.numpy as jnp
from jax import lax
from jax.experimental import pallas as pl
from jax.experimental.pallas import tpu as pltpu
from jax.sharding import PartitionSpec as P

SWEEPS = 4
STEP_WEIGHT = 0.5
MESH = pl.DeviceIdType.MESH

RING = 8
LAG_SUM = 2
LAG_RELAY = 4
LAG_GRAD = 4
EXTRA = 2
FIRST_CHUNK = 3
GROUPS = 2


def kernel(x_hbm, y_hbm, w0_hbm, w0b_hbm, eta_hbm, lam_hbm, w_out, r_out,
           xb, sb, gb, gr, wb, eb, lb, rb, rt, ub, ur, fr,
           x_sem, in_sem, us_sem, ur_sem, rs_sem, rr_sem, lo_sem, gs_sem, gr_sem, ss_sem, sr_sem, wo_sem):
    problem, samp, feat = lax.axis_index("problem"), lax.axis_index("samp"), lax.axis_index("feat")
    partner = feat + 1 - 2 * lax.rem(feat, 2)
    mate = lax.rem(feat + 2, 4)
    cross = lax.rem(partner + 2, 4)
    to_partner, to_mate, to_cross = (problem, samp, partner), (problem, samp, mate), (problem, samp, cross)
    other = 1 - samp
    to_other = (problem, other, feat)

    owned = rb.shape[2]
    tile_rows = 4 * owned
    tiles = rb.shape[1]
    width = gb.shape[2]
    chunks = gr.shape[1]
    chunk = gb.shape[3]
    half_feats = chunks * chunk
    phases = GROUPS * (SWEEPS + 1)
    steps = tiles + EXTRA
    grad_end = tiles - 1 + LAG_GRAD
    total_rows = 2 * tiles * tile_rows

    def remote(src, dst, send, recv, device):
        return pltpu.make_async_remote_copy(src_ref=src, dst_ref=dst, send_sem=send, recv_sem=recv, device_id=device, device_id_type=MESH)

    barrier = pltpu.get_barrier_semaphore()
    for device in (to_partner, to_mate, to_cross, to_other):
        pl.semaphore_signal(barrier, inc=1, device_id=device, device_id_type=MESH)

    def load_tile(tile, slot):
        rows = pl.ds(pl.multiple_of(tile * tile_rows, tile_rows), tile_rows)
        return pltpu.make_async_copy(x_hbm.at[rows], xb.at[slot], x_sem.at[slot])

    own_feats = pl.ds(pl.multiple_of(samp * half_feats, half_feats), half_feats)
    first = [pltpu.make_async_copy(w0b_hbm.at[:, pl.ds(g * width, width)], sb.at[g], in_sem.at[g]) for g in range(GROUPS)]
    rest = [
        pltpu.make_async_copy(y_hbm.at[:, feat, :, pl.ds(g * width, width)], rb.at[g], in_sem.at[GROUPS + g])
        for g in range(GROUPS)
    ]
    rest += [
        pltpu.make_async_copy(w0_hbm.at[own_feats, pl.ds(g * width, width)], wb.at[g], in_sem.at[2 * GROUPS + g])
        for g in range(GROUPS)
    ]
    rest.append(pltpu.make_async_copy(eta_hbm.at[pl.ds(samp * chunks, chunks)], eb, in_sem.at[3 * GROUPS]))
    rest.append(pltpu.make_async_copy(lam_hbm, lb, in_sem.at[3 * GROUPS + 1]))
    first[0].start()
    load_tile(0, 0).start()
    for copy in first[1:] + rest:
        copy.start()
    for slot in range(1, RING):
        load_tile(slot, slot).start()
    for copy in first + rest:
        copy.wait()
    pl.semaphore_wait(barrier, 4)

    def product_copies(slot):
        return [
            remote(ub.at[slot, owner], ur.at[slot, rel], us_sem.at[slot, rel], ur_sem.at[slot, rel], device)
            for rel, (owner, device) in enumerate(((mate, to_mate), (cross, to_cross), (partner, to_partner)))
        ]

    def resid_rows(tile, owner, group):
        return r_out.at[
            pl.ds(pl.multiple_of(tile * tile_rows + owner * owned, owned), owned),
            pl.ds(pl.multiple_of(group * width, width), width),
        ]

    def resid_mate(slot):
        return remote(rt.at[slot, feat], rt.at[slot, feat], rs_sem.at[slot, 0], rr_sem.at[slot, 0], to_mate)

    def resid_partner(slot):
        return remote(rt.at[slot, feat], rt.at[slot, feat], rs_sem.at[slot, 1], rr_sem.at[slot, 1], to_partner)

    def resid_relay(slot):
        return remote(rt.at[slot, mate], rt.at[slot, mate], rs_sem.at[slot, 2], rr_sem.at[slot, 2], to_partner)

    def last_mate(slot, group, tile):
        return remote(rb.at[group, tile], fr.at[slot], rs_sem.at[slot, 0], rr_sem.at[slot, 0], to_mate)

    def last_partner(slot, group, tile):
        return remote(rb.at[group, tile], resid_rows(tile, feat, group), rs_sem.at[slot, 1], rr_sem.at[slot, 1], to_partner)

    def last_relay(slot, group, tile):
        return remote(fr.at[slot], resid_rows(tile, mate, group), rs_sem.at[slot, 2], rr_sem.at[slot, 2], to_partner)

    def last_own(slot, group, tile):
        return pltpu.make_async_copy(rb.at[group, tile], resid_rows(tile, feat, group), lo_sem.at[slot, 0])

    def last_mates(slot, group, tile):
        return pltpu.make_async_copy(fr.at[slot], resid_rows(tile, mate, group), lo_sem.at[slot, 1])

    def grad_copy(group, index):
        return remote(gb.at[group, other * chunks + index], gr.at[group, index], gs_sem.at[group, index], gr_sem.at[group, index], to_other)

    def delta_copy(group, index, count):
        rows = pl.ds(pl.multiple_of(samp * half_feats + index * chunk, chunk), count * chunk)
        return remote(sb.at[group, rows], sb.at[group, rows], ss_sem.at[group], sr_sem.at[group], to_other)

    def coef_rows(group):
        return w_out.at[own_feats, pl.ds(group * width, width)]

    def coef_remote(group):
        return remote(wb.at[group], coef_rows(group), wo_sem.at[group, 0], wo_sem.at[group, 1], to_other)

    def coef_local(group):
        return pltpu.make_async_copy(wb.at[group], coef_rows(group), wo_sem.at[group, 2])

    def step(g, carry):
        def at_lag(lag):
            moved = jnp.maximum(g - lag, 0)
            phase, tile = lax.div(moved, steps), lax.rem(moved, steps)
            active = (g >= lag) & (tile < tiles) & (phase < phases)
            slot = lax.rem(phase * tiles + tile, RING)
            return active, phase, lax.rem(phase, GROUPS), tile, slot

        moved = jnp.maximum(g - grad_end - FIRST_CHUNK, 0)
        chunk_phase, turn = lax.div(moved, steps), lax.rem(moved, steps)
        index = 3 * lax.div(turn, 4) + lax.rem(turn, 4)

        @pl.when((g >= grad_end + FIRST_CHUNK) & (chunk_phase < phases - GROUPS) & (lax.rem(turn, 4) < 3) & (index < chunks))
        def _():
            group = lax.rem(chunk_phase, GROUPS)
            grad_copy(group, index).wait()
            summed = gb[group, samp * chunks + index] + gr[group, index]
            gradient = summed.T * (1.0 / total_rows)
            rows = pl.ds(pl.multiple_of(index * chunk, chunk), chunk)
            coef = wb[group, rows]
            rate = jnp.broadcast_to(eb[index], (width, chunk)).T
            delta = rate * (gradient - lb[group] * coef)
            wb[group, rows] = coef + STEP_WEIGHT * delta
            sb[group, pl.ds(pl.multiple_of(samp * half_feats + index * chunk, chunk), chunk)] = delta.astype(jnp.bfloat16)
            delta_copy(group, index, 1).start()

            @pl.when((chunk_phase == phases - GROUPS - 1) & (index == chunks - 1))
            def _():
                for each in range(GROUPS):
                    coef_remote(each).start()
                    coef_local(each).start()

        active, phase, group, tile, slot = at_lag(LAG_RELAY)
        final = phase >= phases - GROUPS

        @pl.when(active & jnp.logical_not(final))
        def _():
            resid_mate(slot).wait_recv()
            resid_relay(slot).start()

        @pl.when(active & final)
        def _():
            last_mate(slot, group, tile).wait_recv()
            last_relay(slot, group, tile).start()
            last_mates(slot, group, tile).start()

        active_s, phase_s, group_s, tile_s, slot_s = at_lag(LAG_SUM)

        @pl.when(active_s)
        def _():
            for copy in product_copies(slot_s):
                copy.wait_recv()
            summed = ub[slot_s, feat].astype(jnp.float32) + ur[slot_s, 2].astype(jnp.float32)
            summed = summed + (ur[slot_s, 0].astype(jnp.float32) + ur[slot_s, 1].astype(jnp.float32))
            weight = jnp.where(phase_s < GROUPS, 1.0, STEP_WEIGHT)
            resid = rb[group_s, tile_s] - weight * summed
            rb[group_s, tile_s] = resid
            final_s = phase_s >= phases - GROUPS

            @pl.when(jnp.logical_not(final_s))
            def _():
                rt[slot_s, feat] = resid.astype(jnp.bfloat16).T
                resid_mate(slot_s).start()
                resid_partner(slot_s).start()

            @pl.when(final_s)
            def _():
                last_mate(slot_s, group_s, tile_s).start()
                last_partner(slot_s, group_s, tile_s).start()
                last_own(slot_s, group_s, tile_s).start()

        active_x, phase_x, group_x, tile_x, slot_x = at_lag(0)

        @pl.when(active_x & (tile_x == 0) & (phase_x >= GROUPS))
        def _():
            delta_copy(group_x, 0, chunks).wait()

        @pl.when(active_x)
        def _():
            load_tile(tile_x, slot_x).wait()
            product = jnp.dot(xb[slot_x], sb[group_x], preferred_element_type=jnp.float32)
            ub[slot_x] = product.astype(jnp.bfloat16).reshape(4, owned, width)
            for copy in product_copies(slot_x):
                copy.start()

        active_g, phase_g, group_g, tile_g, slot_g = at_lag(LAG_GRAD)
        final_g = phase_g >= phases - GROUPS

        @pl.when(active_g & jnp.logical_not(final_g))
        def _():
            resid_partner(slot_g).wait_recv()
            resid_relay(slot_g).wait_recv()
            left = jnp.concatenate([rt[slot_g, owner] for owner in range(4)], axis=1)
            for each in range(2 * chunks):
                part = jnp.dot(left, xb[slot_g, :, each * chunk:(each + 1) * chunk], preferred_element_type=jnp.float32)
                gb[group_g, each] = jnp.where(tile_g == 0, 0.0, gb[group_g, each]) + part

            @pl.when(tile_g == tiles - 1)
            def _():
                for each in range(chunks):
                    grad_copy(group_g, each).start()

            resid_mate(slot_g).wait_send()
            resid_partner(slot_g).wait_send()
            resid_relay(slot_g).wait_send()

        @pl.when(active_g & final_g)
        def _():
            last_partner(slot_g, group_g, tile_g).wait()
            last_relay(slot_g, group_g, tile_g).wait()
            last_mate(slot_g, group_g, tile_g).wait_send()
            last_own(slot_g, group_g, tile_g).wait()
            last_mates(slot_g, group_g, tile_g).wait()

        @pl.when(active_g)
        def _():
            for copy in product_copies(slot_g):
                copy.wait_send()
            ahead = phase_g * tiles + tile_g + RING

            @pl.when(ahead < phases * tiles)
            def _():
                load_tile(lax.rem(ahead, tiles), slot_g).start()

        return carry

    lax.fori_loop(0, (phases - 1) * steps + tiles + LAG_GRAD, step, 0)
    for group in range(GROUPS):
        coef_remote(group).wait()
        coef_local(group).wait()


def sweeps(design, targets, coef_init, step_sizes, ridge_weights):
    rows, feats = design.shape
    width = targets.shape[1] // GROUPS
    owned = 128
    tiles = rows // (4 * owned)
    chunks = 8
    chunk = feats // (2 * chunks)
    dma = pltpu.SemaphoreType.DMA
    f32, bf16 = jnp.float32, jnp.bfloat16
    scratch = [
        pltpu.VMEM((RING, 4 * owned, feats), bf16),
        pltpu.VMEM((GROUPS, feats, width), bf16),
        pltpu.VMEM((GROUPS, 2 * chunks, width, chunk), f32),
        pltpu.VMEM((GROUPS, chunks, width, chunk), f32),
        pltpu.VMEM((GROUPS, feats // 2, width), f32),
        pltpu.VMEM((chunks, 1, chunk), f32),
        pltpu.VMEM((GROUPS, 1, width), f32),
        pltpu.VMEM((GROUPS, tiles, owned, width), f32),
        pltpu.VMEM((RING, 4, width, owned), bf16),
        pltpu.VMEM((RING, 4, owned, width), bf16),
        pltpu.VMEM((RING, 3, owned, width), bf16),
        pltpu.VMEM((RING, owned, width), f32),
        dma((RING,)),
        dma((3 * GROUPS + 2,)),
        dma((RING, 3)),
        dma((RING, 3)),
        dma((RING, 3)),
        dma((RING, 3)),
        dma((RING, 2)),
        dma((GROUPS, chunks)),
        dma((GROUPS, chunks)),
        dma((GROUPS,)),
        dma((GROUPS,)),
        dma((GROUPS, 3)),
    ]
    return pl.pallas_call(
        kernel,
        out_shape=(jax.ShapeDtypeStruct(coef_init.shape, f32), jax.ShapeDtypeStruct(targets.shape, f32)),
        in_specs=[pl.BlockSpec(memory_space=pl.ANY)] * 6,
        out_specs=[pl.BlockSpec(memory_space=pl.ANY)] * 2,
        scratch_shapes=scratch,
        compiler_params=pltpu.CompilerParams(collective_id=0, has_side_effects=True, vmem_limit_bytes=60 * 2**20),
    )(
        design,
        targets.reshape(tiles, 4, owned, targets.shape[1]),
        coef_init,
        coef_init.astype(bf16),
        step_sizes.reshape(2 * chunks, 1, chunk),
        ridge_weights.reshape(GROUPS, 1, width),
    )


def solution(mesh):
    design_spec = P(("problem", "samp"), "feat")
    rows_spec = P(("problem", "samp"), None)
    coef_spec = P(("problem", "feat"), None)
    step_spec = P(("problem", "feat"))
    ridge_spec = P("problem")
    return jax.shard_map(sweeps, mesh=mesh, in_specs=(design_spec, rows_spec, coef_spec, step_spec, ridge_spec), out_specs=(coef_spec, rows_spec), check_vma=False)
```

time: 1490 us -> 472 us (0.32)
  waiting for transfers between devices: 1120 us -> 0 us
  Pallas kernels: 0 us -> 458 us
  matrix products: 289 us -> 0 us
  other arithmetic: 49.2 us -> 3.71 us
    psum x9 -> x0, waiting for transfers between devices: 1120 us -> none  [the longest x4 576 us: local_sweeps(): lax.psum(block_product(step_delta), 'feat')]
    pallas_call x0 -> x1, Pallas kernels: none -> 458 us  [sweeps(): pl.pallas_call(kernel, out_shape=(jax.ShapeDtypeStruct(coef_init.shape, f...]
    dot_general x9 -> x0, matrix products: 289 us -> none  [the longest x5 162 us: block_product(): jnp.dot(design, weights.astype(jnp.bfloat16), preferred_element_type=jnp....]
    sub x3 -> x0, other arithmetic: 35.4 us -> none  [the longest x2 25.2 us: local_sweeps(): resid_cur - STEP_WEIGHT * lax.psum(block_product(step_delta), 'feat')]
  transfers between devices with their start and end apart: 9 -> 0, of which waited for: 9 -> 0; matrix products, arithmetic and copies ran while one was open for 2% -> 0% of each run, Pallas kernels for 0% -> 0%
where the time goes in v1:
time: 472 us
  Pallas kernels  458 us (97%)
  local copies, waits for them, and re-layouts  9.55 us (2%)
    pallas_call x1, Pallas kernels, sweeps(): pl.pallas_call(kernel, out_shape=(jax.ShapeDtypeStruct(coef_init.shape, f...  458 us
    unnamed x4, local copies, waits for them, and re-layouts  9.55 us

profile of v1, /device:TPU:0, one launch (start us, length us, event | category | flops | bytes accessed | tf_op | source)
XLA Modules:
  0.0 471.9 jit_solution(15174185095971812899)
XLA Ops:
  0.6 3.7 convert_element_type.3.w0b_hbm
  4.3 458.0 %shard_map.68 = (f32[4096,256]{1,0:T(8,128)}, f32[8192,256]{1,0:T(8,128)}) custom-call(bf16[8192,4096]{1,0:T(8,128)(2,1)} %x_hbm.1, f32[16,4,128,256]{3,2,1,0:T(8,128)} %bitcast.3, f32[4096,256]{1,0:T(8,128)} %w0_hbm.1, bf16[4096,256]{1,0:T(8,128)(2,1)} %convert_element_type.3.w0b_hbm, f32[16,1,256]{2,1,0:T(1,128)} %bitcast.4, f32[2,1,128]{2,1,0:T(1,128)} %bitcast.5), custom_call_target="tpu_custom_call" | custom-call | tf_op jit(solution)/shard_map/pallas_call | solution.py:298
  462.4 0.0 copy-start
  462.4 4.8 %copy.9 = f32[4096,256]{1,0:T(8,128)} copy(f32[4096,256]{1,0:T(8,128)} %get-tuple-element.4) | data formatting | bytes 8388608
  467.2 1.4 copy-done
  468.5 3.4 copy.10
Async XLA Ops:
  462.4 6.2 %copy-start = (f32[8192,256]{1,0:T(8,128)S(1)}, f32[8192,256]{1,0:T(8,128)}, u32[]{:S(2)}) copy-start(f32[8192,256]{1,0:T(8,128)} %get-tuple-element.5) | copy-start | bytes 25165828

commit v2 on v1

--- a/solution.py
+++ b/solution.py
@@ -11,17 +11,18 @@
 STEP_WEIGHT = 0.5
 MESH = pl.DeviceIdType.MESH
 
-RING = 8
-LAG_SUM = 2
-LAG_RELAY = 4
-LAG_GRAD = 4
-EXTRA = 2
-FIRST_CHUNK = 3
+RING = 10
+LAG_SUM = 3
+LAG_RELAY = 7
+LAG_GRAD = 8
+EXTRA = 6
+FIRST_CHUNK = 5
+CHUNK_TURNS = (2, 3)
 GROUPS = 2
 
 
-def kernel(x_hbm, y_hbm, w0_hbm, w0b_hbm, eta_hbm, lam_hbm, w_out, r_out,
-           xb, sb, gb, gr, wb, eb, lb, rb, rt, ub, ur, fr,
+def kernel(x_hbm, y_hbm, w0_hbm, eta_hbm, lam_hbm, w_out, r_out,
+           xb, sb, st, gb, gr, wb, eb, lb, rb, rt, ub, ur, fr,
            x_sem, in_sem, us_sem, ur_sem, rs_sem, rr_sem, lo_sem, gs_sem, gr_sem, ss_sem, sr_sem, wo_sem):
     problem, samp, feat = lax.axis_index("problem"), lax.axis_index("samp"), lax.axis_index("feat")
     partner = feat + 1 - 2 * lax.rem(feat, 2)
@@ -55,24 +56,41 @@
         return pltpu.make_async_copy(x_hbm.at[rows], xb.at[slot], x_sem.at[slot])
 
     own_feats = pl.ds(pl.multiple_of(samp * half_feats, half_feats), half_feats)
-    first = [pltpu.make_async_copy(w0b_hbm.at[:, pl.ds(g * width, width)], sb.at[g], in_sem.at[g]) for g in range(GROUPS)]
+    other_feats = pl.ds(pl.multiple_of(other * half_feats, half_feats), half_feats)
+
+    def own_coef(group):
+        return pltpu.make_async_copy(w0_hbm.at[own_feats, pl.ds(group * width, width)], wb.at[group], in_sem.at[group])
+
+    def other_coef(group):
+        return pltpu.make_async_copy(w0_hbm.at[other_feats, pl.ds(group * width, width)], st, in_sem.at[GROUPS + group])
+
+    def round_coef(group):
+        own_coef(group).wait()
+        other_coef(group).wait()
+        for each in range(chunks):
+            rows = pl.ds(each * chunk, chunk)
+            for start, source in ((samp, wb.at[group]), (other, st)):
+                target = pl.ds(pl.multiple_of(start * half_feats + each * chunk, chunk), chunk)
+                sb[group, target] = source[rows].astype(jnp.bfloat16)
+
     rest = [
-        pltpu.make_async_copy(y_hbm.at[:, feat, :, pl.ds(g * width, width)], rb.at[g], in_sem.at[GROUPS + g])
-        for g in range(GROUPS)
-    ]
-    rest += [
-        pltpu.make_async_copy(w0_hbm.at[own_feats, pl.ds(g * width, width)], wb.at[g], in_sem.at[2 * GROUPS + g])
+        pltpu.make_async_copy(y_hbm.at[:, feat, :, pl.ds(g * width, width)], rb.at[g], in_sem.at[2 * GROUPS + g])
         for g in range(GROUPS)
     ]
     rest.append(pltpu.make_async_copy(eta_hbm.at[pl.ds(samp * chunks, chunks)], eb, in_sem.at[3 * GROUPS]))
     rest.append(pltpu.make_async_copy(lam_hbm, lb, in_sem.at[3 * GROUPS + 1]))
-    first[0].start()
+    own_coef(0).start()
+    other_coef(0).start()
     load_tile(0, 0).start()
-    for copy in first[1:] + rest:
+    load_tile(1, 1).start()
+    for copy in rest:
         copy.start()
-    for slot in range(1, RING):
+    own_coef(1).start()
+    for slot in range(2, RING):
         load_tile(slot, slot).start()
-    for copy in first + rest:
+    round_coef(0)
+    other_coef(1).start()
+    for copy in rest:
         copy.wait()
     pl.semaphore_wait(barrier, 4)
 
@@ -136,11 +154,68 @@
             slot = lax.rem(phase * tiles + tile, RING)
             return active, phase, lax.rem(phase, GROUPS), tile, slot
 
+        active_x, phase_x, group_x, tile_x, slot_x = at_lag(0)
+
+        @pl.when(active_x & (tile_x == 0) & (phase_x >= GROUPS))
+        def _():
+            delta_copy(group_x, 0, chunks).wait()
+
+        @pl.when(active_x & (tile_x == 0) & (phase_x == 1))
+        def _():
+            round_coef(1)
+
+        @pl.when(active_x)
+        def _():
+            load_tile(tile_x, slot_x).wait()
+            product = jnp.dot(xb[slot_x], sb[group_x], preferred_element_type=jnp.float32)
+            ub[slot_x] = product.astype(jnp.bfloat16).reshape(4, owned, width)
+            for copy in product_copies(slot_x):
+                copy.start()
+
+        active, phase, group, tile, slot = at_lag(LAG_RELAY)
+        final = phase >= phases - GROUPS
+
+        @pl.when(active & jnp.logical_not(final))
+        def _():
+            resid_mate(slot).wait_recv()
+            resid_relay(slot).start()
+
+        @pl.when(active & final)
+        def _():
+            last_mate(slot, group, tile).wait_recv()
+            last_relay(slot, group, tile).start()
+            last_mates(slot, group, tile).start()
+
+        active_s, phase_s, group_s, tile_s, slot_s = at_lag(LAG_SUM)
+
+        @pl.when(active_s)
+        def _():
+            for copy in product_copies(slot_s):
+                copy.wait_recv()
+            summed = ub[slot_s, feat].astype(jnp.float32) + ur[slot_s, 2].astype(jnp.float32)
+            summed = summed + (ur[slot_s, 0].astype(jnp.float32) + ur[slot_s, 1].astype(jnp.float32))
+            weight = jnp.where(phase_s < GROUPS, 1.0, STEP_WEIGHT)
+            resid = rb[group_s, tile_s] - weight * summed
+            rb[group_s, tile_s] = resid
+            final_s = phase_s >= phases - GROUPS
+
+            @pl.when(jnp.logical_not(final_s))
+            def _():
+                rt[slot_s, feat] = resid.astype(jnp.bfloat16).T
+                resid_mate(slot_s).start()
+                resid_partner(slot_s).start()
+
+            @pl.when(final_s)
+            def _():
+                last_mate(slot_s, group_s, tile_s).start()
+                last_partner(slot_s, group_s, tile_s).start()
+                last_own(slot_s, group_s, tile_s).start()
+
         moved = jnp.maximum(g - grad_end - FIRST_CHUNK, 0)
         chunk_phase, turn = lax.div(moved, steps), lax.rem(moved, steps)
-        index = 3 * lax.div(turn, 4) + lax.rem(turn, 4)
-
-        @pl.when((g >= grad_end + FIRST_CHUNK) & (chunk_phase < phases - GROUPS) & (lax.rem(turn, 4) < 3) & (index < chunks))
+        index = CHUNK_TURNS[0] * lax.div(turn, CHUNK_TURNS[1]) + lax.rem(turn, CHUNK_TURNS[1])
+
+        @pl.when((g >= grad_end + FIRST_CHUNK) & (chunk_phase < phases - GROUPS) & (lax.rem(turn, CHUNK_TURNS[1]) < CHUNK_TURNS[0]) & (index < chunks))
         def _():
             group = lax.rem(chunk_phase, GROUPS)
             grad_copy(group, index).wait()
@@ -159,59 +234,6 @@
                 for each in range(GROUPS):
                     coef_remote(each).start()
                     coef_local(each).start()
-
-        active, phase, group, tile, slot = at_lag(LAG_RELAY)
-        final = phase >= phases - GROUPS
-
-        @pl.when(active & jnp.logical_not(final))
-        def _():
-            resid_mate(slot).wait_recv()
-            resid_relay(slot).start()
-
-        @pl.when(active & final)
-        def _():
-            last_mate(slot, group, tile).wait_recv()
-            last_relay(slot, group, tile).start()
-            last_mates(slot, group, tile).start()
-
-        active_s, phase_s, group_s, tile_s, slot_s = at_lag(LAG_SUM)
-
-        @pl.when(active_s)
-        def _():
-            for copy in product_copies(slot_s):
-                copy.wait_recv()
-            summed = ub[slot_s, feat].astype(jnp.float32) + ur[slot_s, 2].astype(jnp.float32)
-            summed = summed + (ur[slot_s, 0].astype(jnp.float32) + ur[slot_s, 1].astype(jnp.float32))
-            weight = jnp.where(phase_s < GROUPS, 1.0, STEP_WEIGHT)
-            resid = rb[group_s, tile_s] - weight * summed
-            rb[group_s, tile_s] = resid
-            final_s = phase_s >= phases - GROUPS
-
-            @pl.when(jnp.logical_not(final_s))
-            def _():
-                rt[slot_s, feat] = resid.astype(jnp.bfloat16).T
-                resid_mate(slot_s).start()
-                resid_partner(slot_s).start()
-
-            @pl.when(final_s)
-            def _():
-                last_mate(slot_s, group_s, tile_s).start()
-                last_partner(slot_s, group_s, tile_s).start()
-                last_own(slot_s, group_s, tile_s).start()
-
-        active_x, phase_x, group_x, tile_x, slot_x = at_lag(0)
-
-        @pl.when(active_x & (tile_x == 0) & (phase_x >= GROUPS))
-        def _():
-            delta_copy(group_x, 0, chunks).wait()
-
-        @pl.when(active_x)
-        def _():
-            load_tile(tile_x, slot_x).wait()
-            product = jnp.dot(xb[slot_x], sb[group_x], preferred_element_type=jnp.float32)
-            ub[slot_x] = product.astype(jnp.bfloat16).reshape(4, owned, width)
-            for copy in product_copies(slot_x):
-                copy.start()
 
         active_g, phase_g, group_g, tile_g, slot_g = at_lag(LAG_GRAD)
         final_g = phase_g >= phases - GROUPS
@@ -272,6 +294,7 @@
     scratch = [
         pltpu.VMEM((RING, 4 * owned, feats), bf16),
         pltpu.VMEM((GROUPS, feats, width), bf16),
+        pltpu.VMEM((feats // 2, width), f32),
         pltpu.VMEM((GROUPS, 2 * chunks, width, chunk), f32),
         pltpu.VMEM((GROUPS, chunks, width, chunk), f32),
         pltpu.VMEM((GROUPS, feats // 2, width), f32),
@@ -298,15 +321,14 @@
     return pl.pallas_call(
         kernel,
         out_shape=(jax.ShapeDtypeStruct(coef_init.shape, f32), jax.ShapeDtypeStruct(targets.shape, f32)),
-        in_specs=[pl.BlockSpec(memory_space=pl.ANY)] * 6,
+        in_specs=[pl.BlockSpec(memory_space=pl.ANY)] * 5,
         out_specs=[pl.BlockSpec(memory_space=pl.ANY)] * 2,
         scratch_shapes=scratch,
-        compiler_params=pltpu.CompilerParams(collective_id=0, has_side_effects=True, vmem_limit_bytes=60 * 2**20),
+        compiler_params=pltpu.CompilerParams(collective_id=0, has_side_effects=True, vmem_limit_bytes=63 * 2**20),
     )(
         design,
         targets.reshape(tiles, 4, owned, targets.shape[1]),
         coef_init,
-        coef_init.astype(bf16),
         step_sizes.reshape(2 * chunks, 1, chunk),
         ridge_weights.reshape(GROUPS, 1, width),
     )

time: 472 us -> 444 us (0.941)
  Pallas kernels: 458 us -> 433 us
    pallas_call x1, Pallas kernels: 458 us -> 433 us  [sweeps(): pl.pallas_call(kernel, out_shape=(jax.ShapeDtypeStruct(coef_init.shape, f...]
where the time goes in v2:
time: 444 us
  Pallas kernels  433 us (98%)
  local copies, waits for them, and re-layouts  9.55 us (2%)
    pallas_call x1, Pallas kernels, sweeps(): pl.pallas_call(kernel, out_shape=(jax.ShapeDtypeStruct(coef_init.shape, f...  433 us
    unnamed x4, local copies, waits for them, and re-layouts  9.55 us

profile of v2, /device:TPU:0, one launch (start us, length us, event | category | flops | bytes accessed | tf_op | source)
XLA Modules:
  0.0 443.5 jit_solution(10128378571814329811)
XLA Ops:
  0.6 433.3 %shard_map.68 = (f32[4096,256]{1,0:T(8,128)}, f32[8192,256]{1,0:T(8,128)}) custom-call(bf16[8192,4096]{1,0:T(8,128)(2,1)} %x_hbm.1, f32[16,4,128,256]{3,2,1,0:T(8,128)} %bitcast.3, f32[4096,256]{1,0:T(8,128)} %w0_hbm.1, f32[16,1,256]{2,1,0:T(1,128)} %bitcast.4, f32[2,1,128]{2,1,0:T(1,128)} %bitcast.5), custom_call_target="tpu_custom_call" | custom-call | tf_op jit(solution)/shard_map/pallas_call | solution.py:321
  434.0 0.0 copy-start
  434.0 4.8 %copy.9 = f32[4096,256]{1,0:T(8,128)} copy(f32[4096,256]{1,0:T(8,128)} %get-tuple-element.4) | data formatting | bytes 8388608
  438.7 1.4 copy-done
  440.1 3.4 copy.10
Async XLA Ops:
  434.0 6.2 %copy-start = (f32[8192,256]{1,0:T(8,128)S(1)}, f32[8192,256]{1,0:T(8,128)}, u32[]{:S(2)}) copy-start(f32[8192,256]{1,0:T(8,128)} %get-tuple-element.5) | copy-start | bytes 25165828

commit v3 on v1

--- a/solution.py
+++ b/solution.py
@@ -11,17 +11,40 @@
 STEP_WEIGHT = 0.5
 MESH = pl.DeviceIdType.MESH
 
-RING = 8
-LAG_SUM = 2
-LAG_RELAY = 4
-LAG_GRAD = 4
-EXTRA = 2
-FIRST_CHUNK = 3
+RING = 10
+ORDER = "yroxg"
+SWEEP_WORK = "yrgryrgrogrgyorggorgrggrxgxxxoxooxyxroxyrxroggyogoxxrxrgrxogyrgoyoooxxox"
+LAST_WORK = "yrgrygryrgroggrogogxxxxrrxgooorgogxyrrroxroxrxgxoyyxoyoggxgorxgxrygxooox"
+BEHIND = {"r": 9, "o": 3, "g": 10, "y": 11, "x": 0}
 GROUPS = 2
 
 
-def kernel(x_hbm, y_hbm, w0_hbm, w0b_hbm, eta_hbm, lam_hbm, w_out, r_out,
-           xb, sb, gb, gr, wb, eb, lb, rb, rt, ub, ur, fr,
+def pack(work):
+    ranks = [ORDER.index(letter) for letter in work]
+    step, words, last = 0, {letter: [0, 0] for letter in ORDER}, -1
+    for rank, letter in zip(ranks, work):
+        if rank <= last:
+            step += 1
+        last = rank
+        words[letter][step // 31] |= 1 << (step % 31)
+    return step + 1, words
+
+
+def count_steps(tiles, chunks, phases, lengths):
+    total = 0
+    for phase in range(phases + 2):
+        work = SWEEP_WORK if phase < phases - GROUPS else LAST_WORK
+        need = {letter: phases * tiles + BEHIND[letter] for letter in "xorg"}
+        need["y"] = (phases - GROUPS) * chunks + BEHIND["y"]
+        done = {letter: min(phase, phases - GROUPS) * SWEEP_WORK.count(letter) + max(phase - phases + GROUPS, 0) * LAST_WORK.count(letter) for letter in need}
+        if all(done[letter] >= need[letter] for letter in need):
+            break
+        total += lengths[phase >= phases - GROUPS]
+    return total
+
+
+def kernel(x_hbm, y_hbm, w0_hbm, eta_hbm, lam_hbm, w_out, r_out,
+           xb, sb, st, gb, gr, wb, eb, lb, rb, rt, ub, ur, fr,
            x_sem, in_sem, us_sem, ur_sem, rs_sem, rr_sem, lo_sem, gs_sem, gr_sem, ss_sem, sr_sem, wo_sem):
     problem, samp, feat = lax.axis_index("problem"), lax.axis_index("samp"), lax.axis_index("feat")
     partner = feat + 1 - 2 * lax.rem(feat, 2)
@@ -39,8 +62,7 @@
     chunk = gb.shape[3]
     half_feats = chunks * chunk
     phases = GROUPS * (SWEEPS + 1)
-    steps = tiles + EXTRA
-    grad_end = tiles - 1 + LAG_GRAD
+    (sweep_steps, sweep_words), (last_steps, last_words) = pack(SWEEP_WORK), pack(LAST_WORK)
     total_rows = 2 * tiles * tile_rows
 
     def remote(src, dst, send, recv, device):
@@ -55,24 +77,41 @@
         return pltpu.make_async_copy(x_hbm.at[rows], xb.at[slot], x_sem.at[slot])
 
     own_feats = pl.ds(pl.multiple_of(samp * half_feats, half_feats), half_feats)
-    first = [pltpu.make_async_copy(w0b_hbm.at[:, pl.ds(g * width, width)], sb.at[g], in_sem.at[g]) for g in range(GROUPS)]
+    other_feats = pl.ds(pl.multiple_of(other * half_feats, half_feats), half_feats)
+
+    def own_coef(group):
+        return pltpu.make_async_copy(w0_hbm.at[own_feats, pl.ds(group * width, width)], wb.at[group], in_sem.at[group])
+
+    def other_coef(group):
+        return pltpu.make_async_copy(w0_hbm.at[other_feats, pl.ds(group * width, width)], st, in_sem.at[GROUPS + group])
+
+    def round_coef(group):
+        own_coef(group).wait()
+        other_coef(group).wait()
+        for each in range(chunks):
+            rows = pl.ds(each * chunk, chunk)
+            for start, source in ((samp, wb.at[group]), (other, st)):
+                target = pl.ds(pl.multiple_of(start * half_feats + each * chunk, chunk), chunk)
+                sb[group, target] = source[rows].astype(jnp.bfloat16)
+
     rest = [
-        pltpu.make_async_copy(y_hbm.at[:, feat, :, pl.ds(g * width, width)], rb.at[g], in_sem.at[GROUPS + g])
-        for g in range(GROUPS)
-    ]
-    rest += [
-        pltpu.make_async_copy(w0_hbm.at[own_feats, pl.ds(g * width, width)], wb.at[g], in_sem.at[2 * GROUPS + g])
+        pltpu.make_async_copy(y_hbm.at[:, feat, :, pl.ds(g * width, width)], rb.at[g], in_sem.at[2 * GROUPS + g])
         for g in range(GROUPS)
     ]
     rest.append(pltpu.make_async_copy(eta_hbm.at[pl.ds(samp * chunks, chunks)], eb, in_sem.at[3 * GROUPS]))
     rest.append(pltpu.make_async_copy(lam_hbm, lb, in_sem.at[3 * GROUPS + 1]))
-    first[0].start()
+    own_coef(0).start()
+    other_coef(0).start()
     load_tile(0, 0).start()
-    for copy in first[1:] + rest:
+    load_tile(1, 1).start()
+    for copy in rest:
         copy.start()
-    for slot in range(1, RING):
+    own_coef(1).start()
+    for slot in range(2, RING):
         load_tile(slot, slot).start()
-    for copy in first + rest:
+    round_coef(0)
+    other_coef(1).start()
+    for copy in rest:
         copy.wait()
     pl.semaphore_wait(barrier, 4)
 
@@ -128,21 +167,30 @@
     def coef_local(group):
         return pltpu.make_async_copy(wb.at[group], coef_rows(group), wo_sem.at[group, 2])
 
-    def step(g, carry):
-        def at_lag(lag):
-            moved = jnp.maximum(g - lag, 0)
-            phase, tile = lax.div(moved, steps), lax.rem(moved, steps)
-            active = (g >= lag) & (tile < tiles) & (phase < phases)
-            slot = lax.rem(phase * tiles + tile, RING)
-            return active, phase, lax.rem(phase, GROUPS), tile, slot
-
-        moved = jnp.maximum(g - grad_end - FIRST_CHUNK, 0)
-        chunk_phase, turn = lax.div(moved, steps), lax.rem(moved, steps)
-        index = 3 * lax.div(turn, 4) + lax.rem(turn, 4)
-
-        @pl.when((g >= grad_end + FIRST_CHUNK) & (chunk_phase < phases - GROUPS) & (lax.rem(turn, 4) < 3) & (index < chunks))
-        def _():
-            group = lax.rem(chunk_phase, GROUPS)
+    def step(_, carry):
+        turn, period, states = carry
+        ending = period >= phases - GROUPS
+        bits = {}
+        for letter in ORDER:
+            early = jnp.where(ending, jnp.int32(last_words[letter][0]), jnp.int32(sweep_words[letter][0]))
+            late = jnp.where(ending, jnp.int32(last_words[letter][1]), jnp.int32(sweep_words[letter][1]))
+            word = jnp.where(turn < 31, early, late)
+            bits[letter] = lax.shift_right_logical(word, jnp.where(turn < 31, turn, turn - 31)) & 1
+
+        def turn_of(letter):
+            tile, phase, slot = states[letter]
+            active = (bits[letter] == 1) & (tile >= 0) & (phase < phases)
+            return active, phase >= phases - GROUPS, phase, phase & 1, tile, slot
+
+        active_x, _, phase_x, group_x, tile_x, slot_x = turn_of("x")
+        active, final, phase, group, tile, slot = turn_of("r")
+        active_s, final_s, phase_s, group_s, tile_s, slot_s = turn_of("o")
+        active_g, final_g, phase_g, group_g, tile_g, slot_g = turn_of("g")
+        index, chunk_phase, _ = states["y"]
+
+        @pl.when((bits["y"] == 1) & (index >= 0) & (chunk_phase < phases - GROUPS))
+        def _():
+            group = chunk_phase & 1
             grad_copy(group, index).wait()
             summed = gb[group, samp * chunks + index] + gr[group, index]
             gradient = summed.T * (1.0 / total_rows)
@@ -160,9 +208,6 @@
                     coef_remote(each).start()
                     coef_local(each).start()
 
-        active, phase, group, tile, slot = at_lag(LAG_RELAY)
-        final = phase >= phases - GROUPS
-
         @pl.when(active & jnp.logical_not(final))
         def _():
             resid_mate(slot).wait_recv()
@@ -173,8 +218,6 @@
             last_mate(slot, group, tile).wait_recv()
             last_relay(slot, group, tile).start()
             last_mates(slot, group, tile).start()
-
-        active_s, phase_s, group_s, tile_s, slot_s = at_lag(LAG_SUM)
 
         @pl.when(active_s)
         def _():
@@ -185,7 +228,6 @@
             weight = jnp.where(phase_s < GROUPS, 1.0, STEP_WEIGHT)
             resid = rb[group_s, tile_s] - weight * summed
             rb[group_s, tile_s] = resid
-            final_s = phase_s >= phases - GROUPS
 
             @pl.when(jnp.logical_not(final_s))
             def _():
@@ -199,11 +241,13 @@
                 last_partner(slot_s, group_s, tile_s).start()
                 last_own(slot_s, group_s, tile_s).start()
 
-        active_x, phase_x, group_x, tile_x, slot_x = at_lag(0)
-
         @pl.when(active_x & (tile_x == 0) & (phase_x >= GROUPS))
         def _():
             delta_copy(group_x, 0, chunks).wait()
+
+        @pl.when(active_x & (tile_x == 0) & (phase_x == 1))
+        def _():
+            round_coef(1)
 
         @pl.when(active_x)
         def _():
@@ -213,22 +257,29 @@
             for copy in product_copies(slot_x):
                 copy.start()
 
-        active_g, phase_g, group_g, tile_g, slot_g = at_lag(LAG_GRAD)
-        final_g = phase_g >= phases - GROUPS
-
         @pl.when(active_g & jnp.logical_not(final_g))
         def _():
             resid_partner(slot_g).wait_recv()
             resid_relay(slot_g).wait_recv()
-            left = jnp.concatenate([rt[slot_g, owner] for owner in range(4)], axis=1)
-            for each in range(2 * chunks):
-                part = jnp.dot(left, xb[slot_g, :, each * chunk:(each + 1) * chunk], preferred_element_type=jnp.float32)
-                gb[group_g, each] = jnp.where(tile_g == 0, 0.0, gb[group_g, each]) + part
+
+            @pl.when(tile_g < tiles - 1)
+            def _():
+                left = jnp.concatenate([rt[slot_g, owner] for owner in range(4)], axis=1)
+                for each in range(2 * chunks):
+                    share = jnp.dot(left, xb[slot_g, :, each * chunk:(each + 1) * chunk], preferred_element_type=jnp.float32)
+                    gb[group_g, each] = jnp.where(tile_g == 0, 0.0, gb[group_g, each]) + share
 
             @pl.when(tile_g == tiles - 1)
             def _():
-                for each in range(chunks):
-                    grad_copy(group_g, each).start()
+                left = jnp.concatenate([rt[slot_g, owner] for owner in range(4)], axis=1)
+                for side in (other, samp):
+                    for each in range(chunks):
+                        feats = pl.ds(pl.multiple_of((side * chunks + each) * chunk, chunk), chunk)
+                        share = jnp.dot(left, xb[slot_g, :, feats], preferred_element_type=jnp.float32)
+                        gb[group_g, side * chunks + each] += share
+                    if side is other:
+                        for each in range(chunks):
+                            grad_copy(group_g, each).start()
 
             resid_mate(slot_g).wait_send()
             resid_partner(slot_g).wait_send()
@@ -246,15 +297,29 @@
         def _():
             for copy in product_copies(slot_g):
                 copy.wait_send()
-            ahead = phase_g * tiles + tile_g + RING
-
-            @pl.when(ahead < phases * tiles)
-            def _():
-                load_tile(lax.rem(ahead, tiles), slot_g).start()
-
-        return carry
-
-    lax.fori_loop(0, (phases - 1) * steps + tiles + LAG_GRAD, step, 0)
+
+            @pl.when(phase_g * tiles + tile_g + RING < phases * tiles)
+            def _():
+                ahead = jnp.where(tile_g + RING >= tiles, tile_g + RING - tiles, tile_g + RING)
+                load_tile(ahead, slot_g).start()
+
+        following = {}
+        for letter in ORDER:
+            tile, phase, slot = states[letter]
+            slot = jnp.where((bits[letter] == 1) & (tile >= 0), slot + 1, slot)
+            tile = tile + bits[letter]
+            wrap = tile == (chunks if letter == "y" else tiles)
+            following[letter] = (
+                jnp.where(wrap, 0, tile),
+                jnp.where(wrap, phase + 1, phase),
+                jnp.where(slot == RING, 0, slot),
+            )
+        wrap = turn == jnp.where(ending, last_steps - 1, sweep_steps - 1)
+        return jnp.where(wrap, 0, turn + 1), jnp.where(wrap, period + 1, period), following
+
+    zero = jnp.int32(0)
+    start = {letter: (jnp.int32(-BEHIND[letter]), zero, zero) for letter in ORDER}
+    lax.fori_loop(0, count_steps(tiles, chunks, phases, (sweep_steps, last_steps)), step, (zero, zero, start))
     for group in range(GROUPS):
         coef_remote(group).wait()
         coef_local(group).wait()
@@ -272,6 +337,7 @@
     scratch = [
         pltpu.VMEM((RING, 4 * owned, feats), bf16),
         pltpu.VMEM((GROUPS, feats, width), bf16),
+        pltpu.VMEM((feats // 2, width), f32),
         pltpu.VMEM((GROUPS, 2 * chunks, width, chunk), f32),
         pltpu.VMEM((GROUPS, chunks, width, chunk), f32),
         pltpu.VMEM((GROUPS, feats // 2, width), f32),
@@ -298,15 +364,14 @@
     return pl.pallas_call(
         kernel,
         out_shape=(jax.ShapeDtypeStruct(coef_init.shape, f32), jax.ShapeDtypeStruct(targets.shape, f32)),
-        in_specs=[pl.BlockSpec(memory_space=pl.ANY)] * 6,
+        in_specs=[pl.BlockSpec(memory_space=pl.ANY)] * 5,
         out_specs=[pl.BlockSpec(memory_space=pl.ANY)] * 2,
         scratch_shapes=scratch,
-        compiler_params=pltpu.CompilerParams(collective_id=0, has_side_effects=True, vmem_limit_bytes=60 * 2**20),
+        compiler_params=pltpu.CompilerParams(collective_id=0, has_side_effects=True, vmem_limit_bytes=63 * 2**20),
     )(
         design,
         targets.reshape(tiles, 4, owned, targets.shape[1]),
         coef_init,
-        coef_init.astype(bf16),
         step_sizes.reshape(2 * chunks, 1, chunk),
         ridge_weights.reshape(GROUPS, 1, width),
     )

time: 472 us -> 455 us (0.964)
  Pallas kernels: 458 us -> 444 us
    pallas_call x1, Pallas kernels: 458 us -> 444 us  [sweeps(): pl.pallas_call(kernel, out_shape=(jax.ShapeDtypeStruct(coef_init.shape, f...]
where the time goes in v3:
time: 455 us; the launch traced here: 454 us
  Pallas kernels  444 us (98%)
  local copies, waits for them, and re-layouts  9.55 us (2%)
    pallas_call x1, Pallas kernels, sweeps(): pl.pallas_call(kernel, out_shape=(jax.ShapeDtypeStruct(coef_init.shape, f...  444 us
    unnamed x4, local copies, waits for them, and re-layouts  9.55 us

profile of v3, /device:TPU:0, one launch (start us, length us, event | category | flops | bytes accessed | tf_op | source)
XLA Modules:
  0.0 454.4 jit_solution(2743415443935317375)
XLA Ops:
  0.6 444.2 %shard_map.68 = (f32[4096,256]{1,0:T(8,128)}, f32[8192,256]{1,0:T(8,128)}) custom-call(bf16[8192,4096]{1,0:T(8,128)(2,1)} %x_hbm.1, f32[16,4,128,256]{3,2,1,0:T(8,128)} %bitcast.3, f32[4096,256]{1,0:T(8,128)} %w0_hbm.1, f32[16,1,256]{2,1,0:T(1,128)} %bitcast.4, f32[2,1,128]{2,1,0:T(1,128)} %bitcast.5), custom_call_target="tpu_custom_call" | custom-call | tf_op jit(solution)/shard_map/pallas_call | solution.py:364
  444.9 0.0 copy-start
  444.9 4.8 %copy.9 = f32[4096,256]{1,0:T(8,128)} copy(f32[4096,256]{1,0:T(8,128)} %get-tuple-element.4) | data formatting | bytes 8388608
  449.6 1.4 copy-done
  451.0 3.4 copy.10
Async XLA Ops:
  444.9 6.2 %copy-start = (f32[8192,256]{1,0:T(8,128)S(1)}, f32[8192,256]{1,0:T(8,128)}, u32[]{:S(2)}) copy-start(f32[8192,256]{1,0:T(8,128)} %get-tuple-element.5) | copy-start | bytes 25165828

commit v4 on v2

--- a/solution.py
+++ b/solution.py
@@ -16,8 +16,9 @@
 LAG_RELAY = 7
 LAG_GRAD = 8
 EXTRA = 6
-FIRST_CHUNK = 5
-CHUNK_TURNS = (2, 3)
+EXTRA_LAST = 2
+FIRST_CHUNK = 7
+CHUNK_TURNS = (3, 4)
 GROUPS = 2
 
 
@@ -40,7 +41,7 @@
     chunk = gb.shape[3]
     half_feats = chunks * chunk
     phases = GROUPS * (SWEEPS + 1)
-    steps = tiles + EXTRA
+    steps, short = tiles + EXTRA, tiles + EXTRA_LAST
     grad_end = tiles - 1 + LAG_GRAD
     total_rows = 2 * tiles * tile_rows
 
@@ -96,9 +97,12 @@
 
     def product_copies(slot):
         return [
-            remote(ub.at[slot, owner], ur.at[slot, rel], us_sem.at[slot, rel], ur_sem.at[slot, rel], device)
+            remote(ub.at[slot, owner], ur.at[slot, rel], us_sem.at[slot], ur_sem.at[slot], device)
             for rel, (owner, device) in enumerate(((mate, to_mate), (cross, to_cross), (partner, to_partner)))
         ]
+
+    def products(slot):
+        return remote(ur.at[slot], ur.at[slot], us_sem.at[slot], ur_sem.at[slot], to_partner)
 
     def resid_rows(tile, owner, group):
         return r_out.at[
@@ -110,10 +114,16 @@
         return remote(rt.at[slot, feat], rt.at[slot, feat], rs_sem.at[slot, 0], rr_sem.at[slot, 0], to_mate)
 
     def resid_partner(slot):
-        return remote(rt.at[slot, feat], rt.at[slot, feat], rs_sem.at[slot, 1], rr_sem.at[slot, 1], to_partner)
+        return remote(rt.at[slot, feat], rt.at[slot, feat], rs_sem.at[slot, 0], rr_sem.at[slot, 1], to_partner)
 
     def resid_relay(slot):
-        return remote(rt.at[slot, mate], rt.at[slot, mate], rs_sem.at[slot, 2], rr_sem.at[slot, 2], to_partner)
+        return remote(rt.at[slot, mate], rt.at[slot, mate], rs_sem.at[slot, 0], rr_sem.at[slot, 1], to_partner)
+
+    def resid_received(slot):
+        return remote(rt.at[slot, pl.ds(0, 2)], rt.at[slot, pl.ds(0, 2)], rs_sem.at[slot, 0], rr_sem.at[slot, 1], to_partner)
+
+    def resid_sent(slot):
+        return remote(rt.at[slot, pl.ds(0, 3)], rt.at[slot, pl.ds(0, 3)], rs_sem.at[slot, 0], rr_sem.at[slot, 1], to_partner)
 
     def last_mate(slot, group, tile):
         return remote(rb.at[group, tile], fr.at[slot], rs_sem.at[slot, 0], rr_sem.at[slot, 0], to_mate)
@@ -146,34 +156,23 @@
     def coef_local(group):
         return pltpu.make_async_copy(wb.at[group], coef_rows(group), wo_sem.at[group, 2])
 
-    def step(g, carry):
-        def at_lag(lag):
-            moved = jnp.maximum(g - lag, 0)
-            phase, tile = lax.div(moved, steps), lax.rem(moved, steps)
-            active = (g >= lag) & (tile < tiles) & (phase < phases)
-            slot = lax.rem(phase * tiles + tile, RING)
-            return active, phase, lax.rem(phase, GROUPS), tile, slot
-
-        active_x, phase_x, group_x, tile_x, slot_x = at_lag(0)
-
-        @pl.when(active_x & (tile_x == 0) & (phase_x >= GROUPS))
-        def _():
-            delta_copy(group_x, 0, chunks).wait()
-
-        @pl.when(active_x & (tile_x == 0) & (phase_x == 1))
-        def _():
-            round_coef(1)
-
-        @pl.when(active_x)
-        def _():
-            load_tile(tile_x, slot_x).wait()
-            product = jnp.dot(xb[slot_x], sb[group_x], preferred_element_type=jnp.float32)
-            ub[slot_x] = product.astype(jnp.bfloat16).reshape(4, owned, width)
-            for copy in product_copies(slot_x):
-                copy.start()
-
-        active, phase, group, tile, slot = at_lag(LAG_RELAY)
-        final = phase >= phases - GROUPS
+    def step(_, states):
+        def turn_of(name):
+            tile, phase, slot = states[name]
+            active = (tile >= 0) & (tile < tiles) & (phase < phases)
+            return active, phase >= phases - GROUPS, phase, phase & 1, tile, slot
+
+        active_x, _, phase_x, group_x, tile_x, slot_x = turn_of("product")
+        active, final, phase, group, tile, slot = turn_of("relay")
+        active_s, final_s, phase_s, group_s, tile_s, slot_s = turn_of("sum")
+        active_g, final_g, phase_g, group_g, tile_g, slot_g = turn_of("grad")
+        turn, chunk_phase, _ = states["chunk"]
+        if CHUNK_TURNS == (3, 4):
+            part, index = turn & 3, 3 * lax.shift_right_logical(turn, 2) + (turn & 3)
+        elif CHUNK_TURNS == (1, 2):
+            part, index = turn & 1, lax.shift_right_logical(turn, 1)
+        else:
+            part, index = 0, turn
 
         @pl.when(active & jnp.logical_not(final))
         def _():
@@ -186,38 +185,9 @@
             last_relay(slot, group, tile).start()
             last_mates(slot, group, tile).start()
 
-        active_s, phase_s, group_s, tile_s, slot_s = at_lag(LAG_SUM)
-
-        @pl.when(active_s)
-        def _():
-            for copy in product_copies(slot_s):
-                copy.wait_recv()
-            summed = ub[slot_s, feat].astype(jnp.float32) + ur[slot_s, 2].astype(jnp.float32)
-            summed = summed + (ur[slot_s, 0].astype(jnp.float32) + ur[slot_s, 1].astype(jnp.float32))
-            weight = jnp.where(phase_s < GROUPS, 1.0, STEP_WEIGHT)
-            resid = rb[group_s, tile_s] - weight * summed
-            rb[group_s, tile_s] = resid
-            final_s = phase_s >= phases - GROUPS
-
-            @pl.when(jnp.logical_not(final_s))
-            def _():
-                rt[slot_s, feat] = resid.astype(jnp.bfloat16).T
-                resid_mate(slot_s).start()
-                resid_partner(slot_s).start()
-
-            @pl.when(final_s)
-            def _():
-                last_mate(slot_s, group_s, tile_s).start()
-                last_partner(slot_s, group_s, tile_s).start()
-                last_own(slot_s, group_s, tile_s).start()
-
-        moved = jnp.maximum(g - grad_end - FIRST_CHUNK, 0)
-        chunk_phase, turn = lax.div(moved, steps), lax.rem(moved, steps)
-        index = CHUNK_TURNS[0] * lax.div(turn, CHUNK_TURNS[1]) + lax.rem(turn, CHUNK_TURNS[1])
-
-        @pl.when((g >= grad_end + FIRST_CHUNK) & (chunk_phase < phases - GROUPS) & (lax.rem(turn, CHUNK_TURNS[1]) < CHUNK_TURNS[0]) & (index < chunks))
-        def _():
-            group = lax.rem(chunk_phase, GROUPS)
+        @pl.when((turn >= 0) & (chunk_phase < phases - GROUPS) & (part < CHUNK_TURNS[0]) & (index < chunks))
+        def _():
+            group = chunk_phase & 1
             grad_copy(group, index).wait()
             summed = gb[group, samp * chunks + index] + gr[group, index]
             gradient = summed.T * (1.0 / total_rows)
@@ -235,26 +205,58 @@
                     coef_remote(each).start()
                     coef_local(each).start()
 
-        active_g, phase_g, group_g, tile_g, slot_g = at_lag(LAG_GRAD)
-        final_g = phase_g >= phases - GROUPS
-
-        @pl.when(active_g & jnp.logical_not(final_g))
-        def _():
-            resid_partner(slot_g).wait_recv()
-            resid_relay(slot_g).wait_recv()
+        @pl.when(active_x & (tile_x == 0) & (phase_x >= GROUPS))
+        def _():
+            delta_copy(group_x, 0, chunks).wait()
+
+        @pl.when(active_x & (tile_x == 0) & (phase_x == 1))
+        def _():
+            round_coef(1)
+
+        work_g = active_g & jnp.logical_not(final_g)
+
+        def multiply():
+            delta = sb[group_x]
+            product = jnp.dot(xb[slot_x], jnp.concatenate([delta, delta], axis=1), preferred_element_type=jnp.float32)
+            ub[slot_x] = product[:, :width].astype(jnp.bfloat16).reshape(4, owned, width)
+
+        def send():
+            for copy in product_copies(slot_x):
+                copy.start()
+
+        def accumulate():
             left = jnp.concatenate([rt[slot_g, owner] for owner in range(4)], axis=1)
             for each in range(2 * chunks):
-                part = jnp.dot(left, xb[slot_g, :, each * chunk:(each + 1) * chunk], preferred_element_type=jnp.float32)
-                gb[group_g, each] = jnp.where(tile_g == 0, 0.0, gb[group_g, each]) + part
-
+                share = jnp.dot(left, xb[slot_g, :, each * chunk:(each + 1) * chunk], preferred_element_type=jnp.float32)
+                gb[group_g, each] = jnp.where(tile_g == 0, 0.0, gb[group_g, each]) + share
+
+        @pl.when(active_x & work_g)
+        def _():
+            load_tile(tile_x, slot_x).wait()
+            resid_received(slot_g).wait_recv()
+            multiply()
+            accumulate()
+            send()
+
+        @pl.when(active_x & jnp.logical_not(work_g))
+        def _():
+            load_tile(tile_x, slot_x).wait()
+            multiply()
+            send()
+
+        @pl.when(jnp.logical_not(active_x) & work_g)
+        def _():
+            resid_received(slot_g).wait_recv()
+            accumulate()
+
+        @pl.when(work_g)
+        def _():
             @pl.when(tile_g == tiles - 1)
             def _():
                 for each in range(chunks):
                     grad_copy(group_g, each).start()
 
-            resid_mate(slot_g).wait_send()
-            resid_partner(slot_g).wait_send()
-            resid_relay(slot_g).wait_send()
+            resid_sent(slot_g).wait_send()
 
         @pl.when(active_g & final_g)
         def _():
@@ -266,17 +268,50 @@
 
         @pl.when(active_g)
         def _():
-            for copy in product_copies(slot_g):
-                copy.wait_send()
-            ahead = phase_g * tiles + tile_g + RING
-
-            @pl.when(ahead < phases * tiles)
-            def _():
-                load_tile(lax.rem(ahead, tiles), slot_g).start()
-
-        return carry
-
-    lax.fori_loop(0, (phases - 1) * steps + tiles + LAG_GRAD, step, 0)
+            products(slot_g).wait_send()
+
+            @pl.when(phase_g * tiles + tile_g + RING < phases * tiles)
+            def _():
+                ahead = jnp.where(tile_g + RING >= tiles, tile_g + RING - tiles, tile_g + RING)
+                load_tile(ahead, slot_g).start()
+
+        @pl.when(active_s)
+        def _():
+            products(slot_s).wait_recv()
+            summed = ub[slot_s, feat].astype(jnp.float32) + ur[slot_s, 2].astype(jnp.float32)
+            summed = summed + (ur[slot_s, 0].astype(jnp.float32) + ur[slot_s, 1].astype(jnp.float32))
+            weight = jnp.where(phase_s < GROUPS, 1.0, STEP_WEIGHT)
+            resid = rb[group_s, tile_s] - weight * summed
+            rb[group_s, tile_s] = resid
+
+            @pl.when(jnp.logical_not(final_s))
+            def _():
+                rt[slot_s, feat] = resid.astype(jnp.bfloat16).T
+                resid_mate(slot_s).start()
+                resid_partner(slot_s).start()
+
+            @pl.when(final_s)
+            def _():
+                last_mate(slot_s, group_s, tile_s).start()
+                last_partner(slot_s, group_s, tile_s).start()
+                last_own(slot_s, group_s, tile_s).start()
+
+        following = {}
+        for name, (tile, phase, slot) in states.items():
+            within = (tile >= 0) & (tile < tiles)
+            slot = jnp.where(within, slot + 1, slot)
+            wrap = tile == jnp.where(phase == phases - GROUPS, short - 1, steps - 1)
+            following[name] = (
+                jnp.where(wrap, 0, tile + 1),
+                jnp.where(wrap, phase + 1, phase),
+                jnp.where(slot == RING, 0, slot),
+            )
+        return following
+
+    zero = jnp.int32(0)
+    lags = {"product": 0, "sum": LAG_SUM, "relay": LAG_RELAY, "grad": LAG_GRAD, "chunk": grad_end + FIRST_CHUNK}
+    start = {name: (jnp.int32(-lag), zero, zero) for name, lag in lags.items()}
+    lax.fori_loop(0, (phases - 2) * steps + short + tiles + LAG_GRAD, step, start)
     for group in range(GROUPS):
         coef_remote(group).wait()
         coef_local(group).wait()
@@ -307,8 +342,8 @@
         pltpu.VMEM((RING, owned, width), f32),
         dma((RING,)),
         dma((3 * GROUPS + 2,)),
-        dma((RING, 3)),
-        dma((RING, 3)),
+        dma((RING,)),
+        dma((RING,)),
         dma((RING, 3)),
         dma((RING, 3)),
         dma((RING, 2)),

time: 444 us -> 437 us (0.984)
  Pallas kernels: 433 us -> 427 us
    pallas_call x1, Pallas kernels: 433 us -> 427 us  [sweeps(): pl.pallas_call(kernel, out_shape=(jax.ShapeDtypeStruct(coef_init.shape, f...]
where the time goes in v4:
time: 437 us
  Pallas kernels  427 us (98%)
  local copies, waits for them, and re-layouts  9.55 us (2%)
    pallas_call x1, Pallas kernels, sweeps(): pl.pallas_call(kernel, out_shape=(jax.ShapeDtypeStruct(coef_init.shape, f...  427 us
    unnamed x4, local copies, waits for them, and re-layouts  9.55 us

profile of v4, /device:TPU:0, one launch (start us, length us, event | category | flops | bytes accessed | tf_op | source)
XLA Modules:
  0.0 437.1 jit_solution(55672401628768137)
XLA Ops:
  0.6 427.0 %shard_map.68 = (f32[4096,256]{1,0:T(8,128)}, f32[8192,256]{1,0:T(8,128)}) custom-call(bf16[8192,4096]{1,0:T(8,128)(2,1)} %x_hbm.1, f32[16,4,128,256]{3,2,1,0:T(8,128)} %bitcast.3, f32[4096,256]{1,0:T(8,128)} %w0_hbm.1, f32[16,1,256]{2,1,0:T(1,128)} %bitcast.4, f32[2,1,128]{2,1,0:T(1,128)} %bitcast.5), custom_call_target="tpu_custom_call" | custom-call | tf_op jit(solution)/shard_map/pallas_call | solution.py:356
  427.6 0.0 copy-start
  427.6 4.8 %copy.9 = f32[4096,256]{1,0:T(8,128)} copy(f32[4096,256]{1,0:T(8,128)} %get-tuple-element.4) | data formatting | bytes 8388608
  432.4 1.4 copy-done
  433.7 3.4 copy.10
Async XLA Ops:
  427.6 6.2 %copy-start = (f32[8192,256]{1,0:T(8,128)S(1)}, f32[8192,256]{1,0:T(8,128)}, u32[]{:S(2)}) copy-start(f32[8192,256]{1,0:T(8,128)} %get-tuple-element.5) | copy-start | bytes 25165828

commit v5 on v4

--- a/solution.py
+++ b/solution.py
@@ -23,8 +23,8 @@
 
 
 def kernel(x_hbm, y_hbm, w0_hbm, eta_hbm, lam_hbm, w_out, r_out,
-           xb, sb, st, gb, gr, wb, eb, lb, rb, rt, ub, ur, fr,
-           x_sem, in_sem, us_sem, ur_sem, rs_sem, rr_sem, lo_sem, gs_sem, gr_sem, ss_sem, sr_sem, wo_sem):
+           xb, sb, gb, gr, eb, lb, rt, ub, ur,
+           x_sem, in_sem, us_sem, ur_sem, rs_sem, rr_sem, gs_sem, gr_sem, ss_sem, sr_sem, wo_sem):
     problem, samp, feat = lax.axis_index("problem"), lax.axis_index("samp"), lax.axis_index("feat")
     partner = feat + 1 - 2 * lax.rem(feat, 2)
     mate = lax.rem(feat + 2, 4)
@@ -33,9 +33,9 @@
     other = 1 - samp
     to_other = (problem, other, feat)
 
-    owned = rb.shape[2]
+    owned = r_out.shape[2]
     tile_rows = 4 * owned
-    tiles = rb.shape[1]
+    tiles = r_out.shape[0]
     width = gb.shape[2]
     chunks = gr.shape[1]
     chunk = gb.shape[3]
@@ -59,38 +59,32 @@
     own_feats = pl.ds(pl.multiple_of(samp * half_feats, half_feats), half_feats)
     other_feats = pl.ds(pl.multiple_of(other * half_feats, half_feats), half_feats)
 
-    def own_coef(group):
-        return pltpu.make_async_copy(w0_hbm.at[own_feats, pl.ds(group * width, width)], wb.at[group], in_sem.at[group])
-
-    def other_coef(group):
-        return pltpu.make_async_copy(w0_hbm.at[other_feats, pl.ds(group * width, width)], st, in_sem.at[GROUPS + group])
+    def targets_of(group):
+        return pl.ds(pl.multiple_of(group * width, width), width)
+
+    def first_coef(group):
+        return pltpu.make_async_copy(w0_hbm.at[:, targets_of(group)], w_out.at[:, targets_of(group)], in_sem.at[group])
 
     def round_coef(group):
-        own_coef(group).wait()
-        other_coef(group).wait()
-        for each in range(chunks):
+        first_coef(group).wait()
+        for each in range(2 * chunks):
             rows = pl.ds(each * chunk, chunk)
-            for start, source in ((samp, wb.at[group]), (other, st)):
-                target = pl.ds(pl.multiple_of(start * half_feats + each * chunk, chunk), chunk)
-                sb[group, target] = source[rows].astype(jnp.bfloat16)
+            sb[group, rows] = w_out[rows, group * width:(group + 1) * width].astype(jnp.bfloat16)
 
     rest = [
-        pltpu.make_async_copy(y_hbm.at[:, feat, :, pl.ds(g * width, width)], rb.at[g], in_sem.at[2 * GROUPS + g])
-        for g in range(GROUPS)
+        pltpu.make_async_copy(y_hbm.at[:, feat], r_out.at[:, feat], in_sem.at[GROUPS]),
+        pltpu.make_async_copy(eta_hbm.at[pl.ds(samp * chunks, chunks)], eb, in_sem.at[GROUPS + 1]),
+        pltpu.make_async_copy(lam_hbm, lb, in_sem.at[GROUPS + 2]),
     ]
-    rest.append(pltpu.make_async_copy(eta_hbm.at[pl.ds(samp * chunks, chunks)], eb, in_sem.at[3 * GROUPS]))
-    rest.append(pltpu.make_async_copy(lam_hbm, lb, in_sem.at[3 * GROUPS + 1]))
-    own_coef(0).start()
-    other_coef(0).start()
+    first_coef(0).start()
     load_tile(0, 0).start()
     load_tile(1, 1).start()
     for copy in rest:
         copy.start()
-    own_coef(1).start()
+    first_coef(1).start()
     for slot in range(2, RING):
         load_tile(slot, slot).start()
     round_coef(0)
-    other_coef(1).start()
     for copy in rest:
         copy.wait()
     pl.semaphore_wait(barrier, 4)
@@ -104,12 +98,6 @@
     def products(slot):
         return remote(ur.at[slot], ur.at[slot], us_sem.at[slot], ur_sem.at[slot], to_partner)
 
-    def resid_rows(tile, owner, group):
-        return r_out.at[
-            pl.ds(pl.multiple_of(tile * tile_rows + owner * owned, owned), owned),
-            pl.ds(pl.multiple_of(group * width, width), width),
-        ]
-
     def resid_mate(slot):
         return remote(rt.at[slot, feat], rt.at[slot, feat], rs_sem.at[slot, 0], rr_sem.at[slot, 0], to_mate)
 
@@ -125,20 +113,20 @@
     def resid_sent(slot):
         return remote(rt.at[slot, pl.ds(0, 3)], rt.at[slot, pl.ds(0, 3)], rs_sem.at[slot, 0], rr_sem.at[slot, 1], to_partner)
 
+    def last_rows(tile, owner, group):
+        return r_out.at[tile, owner, :, targets_of(group)]
+
     def last_mate(slot, group, tile):
-        return remote(rb.at[group, tile], fr.at[slot], rs_sem.at[slot, 0], rr_sem.at[slot, 0], to_mate)
+        rows = last_rows(tile, feat, group)
+        return remote(rows, rows, rs_sem.at[slot, 0], rr_sem.at[slot, 0], to_mate)
 
     def last_partner(slot, group, tile):
-        return remote(rb.at[group, tile], resid_rows(tile, feat, group), rs_sem.at[slot, 1], rr_sem.at[slot, 1], to_partner)
+        rows = last_rows(tile, feat, group)
+        return remote(rows, rows, rs_sem.at[slot, 1], rr_sem.at[slot, 1], to_partner)
 
     def last_relay(slot, group, tile):
-        return remote(fr.at[slot], resid_rows(tile, mate, group), rs_sem.at[slot, 2], rr_sem.at[slot, 2], to_partner)
-
-    def last_own(slot, group, tile):
-        return pltpu.make_async_copy(rb.at[group, tile], resid_rows(tile, feat, group), lo_sem.at[slot, 0])
-
-    def last_mates(slot, group, tile):
-        return pltpu.make_async_copy(fr.at[slot], resid_rows(tile, mate, group), lo_sem.at[slot, 1])
+        rows = last_rows(tile, mate, group)
+        return remote(rows, rows, rs_sem.at[slot, 2], rr_sem.at[slot, 2], to_partner)
 
     def grad_copy(group, index):
         return remote(gb.at[group, other * chunks + index], gr.at[group, index], gs_sem.at[group, index], gr_sem.at[group, index], to_other)
@@ -147,14 +135,9 @@
         rows = pl.ds(pl.multiple_of(samp * half_feats + index * chunk, chunk), count * chunk)
         return remote(sb.at[group, rows], sb.at[group, rows], ss_sem.at[group], sr_sem.at[group], to_other)
 
-    def coef_rows(group):
-        return w_out.at[own_feats, pl.ds(group * width, width)]
-
-    def coef_remote(group):
-        return remote(wb.at[group], coef_rows(group), wo_sem.at[group, 0], wo_sem.at[group, 1], to_other)
-
-    def coef_local(group):
-        return pltpu.make_async_copy(wb.at[group], coef_rows(group), wo_sem.at[group, 2])
+    def coef_copy(group):
+        rows = w_out.at[own_feats, targets_of(group)]
+        return remote(rows, rows, wo_sem.at[group, 0], wo_sem.at[group, 1], to_other)
 
     def step(_, states):
         def turn_of(name):
@@ -183,7 +166,6 @@
         def _():
             last_mate(slot, group, tile).wait_recv()
             last_relay(slot, group, tile).start()
-            last_mates(slot, group, tile).start()
 
         @pl.when((turn >= 0) & (chunk_phase < phases - GROUPS) & (part < CHUNK_TURNS[0]) & (index < chunks))
         def _():
@@ -191,19 +173,18 @@
             grad_copy(group, index).wait()
             summed = gb[group, samp * chunks + index] + gr[group, index]
             gradient = summed.T * (1.0 / total_rows)
-            rows = pl.ds(pl.multiple_of(index * chunk, chunk), chunk)
-            coef = wb[group, rows]
+            rows = pl.ds(pl.multiple_of(samp * half_feats + index * chunk, chunk), chunk)
+            coef = w_out[rows, targets_of(group)]
             rate = jnp.broadcast_to(eb[index], (width, chunk)).T
             delta = rate * (gradient - lb[group] * coef)
-            wb[group, rows] = coef + STEP_WEIGHT * delta
-            sb[group, pl.ds(pl.multiple_of(samp * half_feats + index * chunk, chunk), chunk)] = delta.astype(jnp.bfloat16)
+            w_out[rows, targets_of(group)] = coef + STEP_WEIGHT * delta
+            sb[group, rows] = delta.astype(jnp.bfloat16)
             delta_copy(group, index, 1).start()
 
             @pl.when((chunk_phase == phases - GROUPS - 1) & (index == chunks - 1))
             def _():
                 for each in range(GROUPS):
-                    coef_remote(each).start()
-                    coef_local(each).start()
+                    coef_copy(each).start()
 
         @pl.when(active_x & (tile_x == 0) & (phase_x >= GROUPS))
         def _():
@@ -263,8 +244,6 @@
             last_partner(slot_g, group_g, tile_g).wait()
             last_relay(slot_g, group_g, tile_g).wait()
             last_mate(slot_g, group_g, tile_g).wait_send()
-            last_own(slot_g, group_g, tile_g).wait()
-            last_mates(slot_g, group_g, tile_g).wait()
 
         @pl.when(active_g)
         def _():
@@ -281,8 +260,8 @@
             summed = ub[slot_s, feat].astype(jnp.float32) + ur[slot_s, 2].astype(jnp.float32)
             summed = summed + (ur[slot_s, 0].astype(jnp.float32) + ur[slot_s, 1].astype(jnp.float32))
             weight = jnp.where(phase_s < GROUPS, 1.0, STEP_WEIGHT)
-            resid = rb[group_s, tile_s] - weight * summed
-            rb[group_s, tile_s] = resid
+            resid = r_out[tile_s, feat, :, targets_of(group_s)] - weight * summed
+            r_out[tile_s, feat, :, targets_of(group_s)] = resid
 
             @pl.when(jnp.logical_not(final_s))
             def _():
@@ -294,7 +273,6 @@
             def _():
                 last_mate(slot_s, group_s, tile_s).start()
                 last_partner(slot_s, group_s, tile_s).start()
-                last_own(slot_s, group_s, tile_s).start()
 
         following = {}
         for name, (tile, phase, slot) in states.items():
@@ -313,8 +291,7 @@
     start = {name: (jnp.int32(-lag), zero, zero) for name, lag in lags.items()}
     lax.fori_loop(0, (phases - 2) * steps + short + tiles + LAG_GRAD, step, start)
     for group in range(GROUPS):
-        coef_remote(group).wait()
-        coef_local(group).wait()
+        coef_copy(group).wait()
 
 
 def sweeps(design, targets, coef_init, step_sizes, ridge_weights):
@@ -329,44 +306,41 @@
     scratch = [
         pltpu.VMEM((RING, 4 * owned, feats), bf16),
         pltpu.VMEM((GROUPS, feats, width), bf16),
-        pltpu.VMEM((feats // 2, width), f32),
         pltpu.VMEM((GROUPS, 2 * chunks, width, chunk), f32),
         pltpu.VMEM((GROUPS, chunks, width, chunk), f32),
-        pltpu.VMEM((GROUPS, feats // 2, width), f32),
         pltpu.VMEM((chunks, 1, chunk), f32),
         pltpu.VMEM((GROUPS, 1, width), f32),
-        pltpu.VMEM((GROUPS, tiles, owned, width), f32),
         pltpu.VMEM((RING, 4, width, owned), bf16),
         pltpu.VMEM((RING, 4, owned, width), bf16),
         pltpu.VMEM((RING, 3, owned, width), bf16),
-        pltpu.VMEM((RING, owned, width), f32),
         dma((RING,)),
-        dma((3 * GROUPS + 2,)),
+        dma((GROUPS + 3,)),
         dma((RING,)),
         dma((RING,)),
         dma((RING, 3)),
         dma((RING, 3)),
-        dma((RING, 2)),
         dma((GROUPS, chunks)),
         dma((GROUPS, chunks)),
         dma((GROUPS,)),
         dma((GROUPS,)),
-        dma((GROUPS, 3)),
+        dma((GROUPS, 2)),
     ]
-    return pl.pallas_call(
+    tiled = (tiles, 4, owned, targets.shape[1])
+    coef, resid = pl.pallas_call(
         kernel,
-        out_shape=(jax.ShapeDtypeStruct(coef_init.shape, f32), jax.ShapeDtypeStruct(targets.shape, f32)),
+        out_shape=(pltpu.VMEM(coef_init.shape, f32), pltpu.VMEM(tiled, f32)),
         in_specs=[pl.BlockSpec(memory_space=pl.ANY)] * 5,
-        out_specs=[pl.BlockSpec(memory_space=pl.ANY)] * 2,
+        out_specs=[pl.BlockSpec(memory_space=pltpu.VMEM)] * 2,
         scratch_shapes=scratch,
-        compiler_params=pltpu.CompilerParams(collective_id=0, has_side_effects=True, vmem_limit_bytes=63 * 2**20),
+        compiler_params=pltpu.CompilerParams(collective_id=0, has_side_effects=True, vmem_limit_bytes=519 * 2**20 // 10),
     )(
         design,
-        targets.reshape(tiles, 4, owned, targets.shape[1]),
+        targets.reshape(tiled),
         coef_init,
         step_sizes.reshape(2 * chunks, 1, chunk),
         ridge_weights.reshape(GROUPS, 1, width),
     )
+    return coef, resid.reshape(targets.shape)
 
 
 def solution(mesh):

time: 437 us -> 433 us (level)
    unnamed x4 -> x2, local copies, waits for them, and re-layouts: 9.55 us -> 5.41 us
where the time goes in v5:
time: 433 us; the launch traced here: 432 us
  Pallas kernels  426 us (98%)
  local copies, waits for them, and re-layouts  5.41 us (1%)
    pallas_call x1, Pallas kernels, sweeps(): pl.pallas_call(kernel, out_shape=(pltpu.VMEM(coef_init.shape, f32), pltpu...  426 us

profile of v5, /device:TPU:0, one launch (start us, length us, event | category | flops | bytes accessed | tf_op | source)
XLA Modules:
  0.0 432.5 jit_solution(16844698537026760511)
XLA Ops:
  0.6 426.4 %shard_map.68 = (f32[4096,256]{1,0:T(8,128)S(1)}, f32[16,4,128,256]{3,2,1,0:T(8,128)S(1)}) custom-call(bf16[8192,4096]{1,0:T(8,128)(2,1)} %x_hbm.1, f32[16,4,128,256]{3,2,1,0:T(8,128)} %bitcast.5, f32[4096,256]{1,0:T(8,128)} %w0_hbm.1, f32[16,1,256]{2,1,0:T(1,128)} %bitcast.6, f32[2,1,128]{2,1,0:T(1,128)} %bitcast.7), custom_call_target="tpu_custom_call" | custom-call | tf_op jit(solution)/shard_map/pallas_call | solution.py:329
  427.1 2.0 copy.9
  429.1 3.4 copy.10

commit v6 on v5

--- a/solution.py
+++ b/solution.py
@@ -12,6 +12,7 @@
 MESH = pl.DeviceIdType.MESH
 
 RING = 10
+AHEAD = 2
 LAG_SUM = 3
 LAG_RELAY = 7
 LAG_GRAD = 8
@@ -78,15 +79,11 @@
     ]
     first_coef(0).start()
     load_tile(0, 0).start()
-    load_tile(1, 1).start()
     for copy in rest:
         copy.start()
-    first_coef(1).start()
-    for slot in range(2, RING):
+    for slot in range(1, AHEAD):
         load_tile(slot, slot).start()
     round_coef(0)
-    for copy in rest:
-        copy.wait()
     pl.semaphore_wait(barrier, 4)
 
     def product_copies(slot):
@@ -194,6 +191,16 @@
         def _():
             round_coef(1)
 
+        @pl.when(active_x & (phase_x == 0))
+        def _():
+            @pl.when(tile_x < RING - AHEAD)
+            def _():
+                load_tile(tile_x + AHEAD, slot_x + AHEAD).start()
+
+            @pl.when(tile_x == RING - AHEAD)
+            def _():
+                first_coef(1).start()
+
         work_g = active_g & jnp.logical_not(final_g)
 
         def multiply():
@@ -253,6 +260,11 @@
             def _():
                 ahead = jnp.where(tile_g + RING >= tiles, tile_g + RING - tiles, tile_g + RING)
                 load_tile(ahead, slot_g).start()
+
+        @pl.when(active_s & (tile_s == 0) & (phase_s == 0))
+        def _():
+            for copy in rest:
+                copy.wait()
 
         @pl.when(active_s)
         def _():

time: 433 us -> 425 us (0.982)
  Pallas kernels: 426 us -> 419 us
    pallas_call x1, Pallas kernels: 426 us -> 419 us  [sweeps(): pl.pallas_call(kernel, out_shape=(pltpu.VMEM(coef_init.shape, f32), pltpu...]
where the time goes in v6:
time: 425 us
  Pallas kernels  419 us (99%)
  local copies, waits for them, and re-layouts  5.41 us (1%)
    pallas_call x1, Pallas kernels, sweeps(): pl.pallas_call(kernel, out_shape=(pltpu.VMEM(coef_init.shape, f32), pltpu...  419 us

profile of v6, /device:TPU:0, one launch (start us, length us, event | category | flops | bytes accessed | tf_op | source)
XLA Modules:
  0.0 424.7 jit_solution(4974447902765037483)
XLA Ops:
  0.6 418.7 %shard_map.68 = (f32[4096,256]{1,0:T(8,128)S(1)}, f32[16,4,128,256]{3,2,1,0:T(8,128)S(1)}) custom-call(bf16[8192,4096]{1,0:T(8,128)(2,1)} %x_hbm.1, f32[16,4,128,256]{3,2,1,0:T(8,128)} %bitcast.5, f32[4096,256]{1,0:T(8,128)} %w0_hbm.1, f32[16,1,256]{2,1,0:T(1,128)} %bitcast.6, f32[2,1,128]{2,1,0:T(1,128)} %bitcast.7), custom_call_target="tpu_custom_call" | custom-call | tf_op jit(solution)/shard_map/pallas_call | solution.py:341
  419.3 2.0 copy.9
  421.3 3.4 copy.10

commit v7 on v6

--- a/solution.py
+++ b/solution.py
@@ -212,13 +212,46 @@
             for copy in product_copies(slot_x):
                 copy.start()
 
+        def left_of(slot):
+            return jnp.concatenate([rt[slot, owner] for owner in range(4)], axis=1)
+
         def accumulate():
-            left = jnp.concatenate([rt[slot_g, owner] for owner in range(4)], axis=1)
+            left = left_of(slot_g)
             for each in range(2 * chunks):
                 share = jnp.dot(left, xb[slot_g, :, each * chunk:(each + 1) * chunk], preferred_element_type=jnp.float32)
                 gb[group_g, each] = jnp.where(tile_g == 0, 0.0, gb[group_g, each]) + share
 
-        @pl.when(active_x & work_g)
+        def retire(slot, tile):
+            products(slot).wait_send()
+
+            @pl.when(phase_g * tiles + tile + RING < phases * tiles)
+            def _():
+                ahead = jnp.where(tile + RING >= tiles, tile + RING - tiles, tile + RING)
+                load_tile(ahead, slot).start()
+
+        slot_b = jnp.where(slot_g == 0, RING - 1, slot_g - 1)
+
+        @pl.when(work_g & (tile_g == tiles - 1))
+        def _():
+            resid_received(slot_b).wait_recv()
+            resid_received(slot_g).wait_recv()
+            left_b, left_g = left_of(slot_b), left_of(slot_g)
+            for side in (other, samp):
+                for each in range(chunks):
+                    feats = pl.ds(pl.multiple_of((side * chunks + each) * chunk, chunk), chunk)
+                    share = jnp.dot(left_b, xb[slot_b, :, feats], preferred_element_type=jnp.float32)
+                    share = share + jnp.dot(left_g, xb[slot_g, :, feats], preferred_element_type=jnp.float32)
+                    gb[group_g, side * chunks + each] += share
+                if side is other:
+                    for each in range(chunks):
+                        grad_copy(group_g, each).start()
+            for slot_each, tile_each in ((slot_b, tile_g - 1), (slot_g, tile_g)):
+                resid_sent(slot_each).wait_send()
+                retire(slot_each, tile_each)
+
+        single_g = work_g & (tile_g < tiles - 2)
+
+        @pl.when(active_x & single_g)
         def _():
             load_tile(tile_x, slot_x).wait()
             resid_received(slot_g).wait_recv()
@@ -226,40 +259,28 @@
             accumulate()
             send()
 
-        @pl.when(active_x & jnp.logical_not(work_g))
+        @pl.when(active_x & jnp.logical_not(single_g))
         def _():
             load_tile(tile_x, slot_x).wait()
             multiply()
             send()
 
-        @pl.when(jnp.logical_not(active_x) & work_g)
+        @pl.when(jnp.logical_not(active_x) & single_g)
         def _():
             resid_received(slot_g).wait_recv()
             accumulate()
 
-        @pl.when(work_g)
-        def _():
-            @pl.when(tile_g == tiles - 1)
-            def _():
-                for each in range(chunks):
-                    grad_copy(group_g, each).start()
-
+        @pl.when(single_g)
+        def _():
             resid_sent(slot_g).wait_send()
+            retire(slot_g, tile_g)
 
         @pl.when(active_g & final_g)
         def _():
             last_partner(slot_g, group_g, tile_g).wait()
             last_relay(slot_g, group_g, tile_g).wait()
             last_mate(slot_g, group_g, tile_g).wait_send()
-
-        @pl.when(active_g)
-        def _():
-            products(slot_g).wait_send()
-
-            @pl.when(phase_g * tiles + tile_g + RING < phases * tiles)
-            def _():
-                ahead = jnp.where(tile_g + RING >= tiles, tile_g + RING - tiles, tile_g + RING)
-                load_tile(ahead, slot_g).start()
+            retire(slot_g, tile_g)
 
         @pl.when(active_s & (tile_s == 0) & (phase_s == 0))
         def _():

time: 425 us -> 427 us (level)
  no operation moved by 1% of the time
where the time goes in v7:
time: 427 us
  Pallas kernels  421 us (99%)
  local copies, waits for them, and re-layouts  5.41 us (1%)
    pallas_call x1, Pallas kernels, sweeps(): pl.pallas_call(kernel, out_shape=(pltpu.VMEM(coef_init.shape, f32), pltpu...  421 us

profile of v7, /device:TPU:0, one launch (start us, length us, event | category | flops | bytes accessed | tf_op | source)
XLA Modules:
  0.0 426.6 jit_solution(11800795058234323229)
XLA Ops:
  0.6 420.5 %shard_map.68 = (f32[4096,256]{1,0:T(8,128)S(1)}, f32[16,4,128,256]{3,2,1,0:T(8,128)S(1)}) custom-call(bf16[8192,4096]{1,0:T(8,128)(2,1)} %x_hbm.1, f32[16,4,128,256]{3,2,1,0:T(8,128)} %bitcast.5, f32[4096,256]{1,0:T(8,128)} %w0_hbm.1, f32[16,1,256]{2,1,0:T(1,128)} %bitcast.6, f32[2,1,128]{2,1,0:T(1,128)} %bitcast.7), custom_call_target="tpu_custom_call" | custom-call | tf_op jit(solution)/shard_map/pallas_call | solution.py:362
  421.2 2.0 copy.9
  423.2 3.4 copy.10

commit v8 on v6

--- a/solution.py
+++ b/solution.py
@@ -20,6 +20,7 @@
 EXTRA_LAST = 2
 FIRST_CHUNK = 7
 CHUNK_TURNS = (3, 4)
+PIECES = 4
 GROUPS = 2
 
 
@@ -79,11 +80,11 @@
     ]
     first_coef(0).start()
     load_tile(0, 0).start()
-    for copy in rest:
-        copy.start()
     for slot in range(1, AHEAD):
         load_tile(slot, slot).start()
     round_coef(0)
+    for copy in rest:
+        copy.start()
     pl.semaphore_wait(barrier, 4)
 
     def product_copies(slot):
@@ -304,6 +305,19 @@
     lax.fori_loop(0, (phases - 2) * steps + short + tiles + LAG_GRAD, step, start)
     for group in range(GROUPS):
         coef_copy(group).wait()
+
+
+def write_out(coef, resid, coef_out, resid_out, sem):
+    copies = []
+    for source, target in ((coef, coef_out), (resid, resid_out)):
+        rows = source.shape[0] // PIECES
+        for piece in range(PIECES):
+            part = pl.ds(piece * rows, rows)
+            copies.append(pltpu.make_async_copy(source.at[part], target.at[part], sem.at[len(copies)]))
+    for copy in copies:
+        copy.start()
+    for copy in copies:
+        copy.wait()
 
 
 def sweeps(design, targets, coef_init, step_sizes, ridge_weights):
@@ -352,6 +366,14 @@
         step_sizes.reshape(2 * chunks, 1, chunk),
         ridge_weights.reshape(GROUPS, 1, width),
     )
+    coef, resid = pl.pallas_call(
+        write_out,
+        out_shape=(jax.ShapeDtypeStruct(coef.shape, f32), jax.ShapeDtypeStruct(tiled, f32)),
+        in_specs=[pl.BlockSpec(memory_space=pl.ANY)] * 2,
+        out_specs=[pl.BlockSpec(memory_space=pl.ANY)] * 2,
+        scratch_shapes=[dma((2 * PIECES,))],
+        compiler_params=pltpu.CompilerParams(vmem_limit_bytes=2**20),
+    )(pltpu.with_memory_space_constraint(coef, pltpu.VMEM), pltpu.with_memory_space_constraint(resid, pltpu.VMEM))
     return coef, resid.reshape(targets.shape)
 
 

time: 425 us -> 424 us (level)
  local copies, waits for them, and re-layouts: 5.41 us -> 0 us
    unnamed x2 -> x0, local copies, waits for them, and re-layouts: 5.41 us -> none
    pallas_call x0 -> x1, Pallas kernels: none -> 4.66 us  [sweeps(): pl.pallas_call(write_out, out_shape=(jax.ShapeDtypeStruct(coef.shape, f32...]
where the time goes in v8:
time: 424 us
  Pallas kernels  423 us (100%)
    pallas_call x1, Pallas kernels, sweeps(): pl.pallas_call(kernel, out_shape=(pltpu.VMEM(coef_init.shape, f32), pltpu...  419 us

profile of v8, /device:TPU:0, one launch (start us, length us, event | category | flops | bytes accessed | tf_op | source)
XLA Modules:
  0.0 423.9 jit_solution(3422558268659769714)
XLA Ops:
  0.6 418.6 %shard_map.68 = (f32[4096,256]{1,0:T(8,128)S(1)}, f32[16,4,128,256]{3,2,1,0:T(8,128)S(1)}) custom-call(bf16[8192,4096]{1,0:T(8,128)(2,1)} %x_hbm.1, f32[16,4,128,256]{3,2,1,0:T(8,128)} %bitcast.4, f32[4096,256]{1,0:T(8,128)} %w0_hbm.1, f32[16,1,256]{2,1,0:T(1,128)} %bitcast.5, f32[2,1,128]{2,1,0:T(1,128)} %bitcast.6), custom_call_target="tpu_custom_call" | custom-call | tf_op jit(solution)/shard_map/pallas_call | solution.py:355
  419.2 4.7 %shard_map.69 = (f32[4096,256]{1,0:T(8,128)}, f32[16,4,128,256]{3,2,1,0:T(8,128)}) custom-call(f32[4096,256]{1,0:T(8,128)S(1)} %get-tuple-element.6.coef, f32[16,4,128,256]{3,2,1,0:T(8,128)S(1)} %get-tuple-element.7.resid), custom_call_target="tpu_custom_call" | custom-call | tf_op jit(solution)/shard_map/pallas_call | solution.py:369

commit v9 on v8

--- a/solution.py
+++ b/solution.py
@@ -16,9 +16,9 @@
 LAG_SUM = 3
 LAG_RELAY = 7
 LAG_GRAD = 8
-EXTRA = 6
+EXTRA = 7
 EXTRA_LAST = 2
-FIRST_CHUNK = 7
+FIRST_CHUNK = 6
 CHUNK_TURNS = (3, 4)
 PIECES = 4
 GROUPS = 2

time: 424 us -> 426 us (level)
  no operation moved by 1% of the time
where the time goes in v9:
time: 426 us
  Pallas kernels  426 us (100%)
    pallas_call x1, Pallas kernels, sweeps(): pl.pallas_call(kernel, out_shape=(pltpu.VMEM(coef_init.shape, f32), pltpu...  421 us

profile of v9, /device:TPU:0, one launch (start us, length us, event | category | flops | bytes accessed | tf_op | source)
XLA Modules:
  0.0 426.3 jit_solution(7153995717901406654)
XLA Ops:
  0.6 421.0 %shard_map.68 = (f32[4096,256]{1,0:T(8,128)S(1)}, f32[16,4,128,256]{3,2,1,0:T(8,128)S(1)}) custom-call(bf16[8192,4096]{1,0:T(8,128)(2,1)} %x_hbm.1, f32[16,4,128,256]{3,2,1,0:T(8,128)} %bitcast.4, f32[4096,256]{1,0:T(8,128)} %w0_hbm.1, f32[16,1,256]{2,1,0:T(1,128)} %bitcast.5, f32[2,1,128]{2,1,0:T(1,128)} %bitcast.6), custom_call_target="tpu_custom_call" | custom-call | tf_op jit(solution)/shard_map/pallas_call | solution.py:355
  421.7 4.7 %shard_map.69 = (f32[4096,256]{1,0:T(8,128)}, f32[16,4,128,256]{3,2,1,0:T(8,128)}) custom-call(f32[4096,256]{1,0:T(8,128)S(1)} %get-tuple-element.6.coef, f32[16,4,128,256]{3,2,1,0:T(8,128)S(1)} %get-tuple-element.7.resid), custom_call_target="tpu_custom_call" | custom-call | tf_op jit(solution)/shard_map/pallas_call | solution.py:369
